TPU v7x, 256 devices: a 2x2x32 block of a 4x8x32 slice. The times are simulated.
256 devices in a mesh: groups: 4 (over y, x), row: 64 (over z, core).
Axes of the slice: x: 2, y: 2, z: 32, core: 2. Of those that a mesh axis runs over, the one named last changes fastest.
The devices are a block of a 4x8x32 slice.
Arguments:
- pair_in: bfloat16 [2048, 512, 128], P(('groups', 'row')), parts along dimension 0, may hold values from -6 to 6
- valid_tokens: int32 [2048], P('groups'), parts along dimension 0, may hold values 0 or 1
- proj_weight: bfloat16 [2, 128, 640], replicated, may hold values from -0.5 to 0.5
- out_weight: bfloat16 [2, 128, 128], replicated, may hold values from -0.5 to 0.5
- norm_gains: float32 [2, 2, 128], replicated, may hold values from 0.1 to 1.9
Outputs:
- pair_out: bfloat16 [2048, 512, 128], P(('groups', 'row')), parts along dimension 0
There are 4 independent parts, one for each index of `groups`. A program takes and returns all parts, laid end to end along the dimension named above; an argument that names none is the same for every part. Nothing has to cross between parts.
All inputs are finite; a program needn't handle non-finite values.
Results may differ from a plain program's by a relative error of at most 0.007.
Values may be sent and summed in bfloat16 or wider, within the bound.
A program may use at most 64 MiB of HBM per device.

v0:
```python
import jax
import jax.numpy as jnp
from jax import lax
from jax.sharding import PartitionSpec as P

EPSILON = 1e-05


def sent_together(arrays, axis, split_dim, concat_dim, along):
    widths = [a.shape[along] for a in arrays]
    both = jnp.concatenate(arrays, axis=along)
    filled = lax.all_to_all(both, axis, split_axis=split_dim, concat_axis=concat_dim, tiled=True)
    return tuple(jnp.split(filled, [sum(widths[:k]) for k in range(1, len(widths))], axis=along))


def layer_norm(values, gain, axis_num):
    mean = jnp.mean(values, axis=axis_num, keepdims=True)
    centered = values - mean
    variance = jnp.mean(centered * centered, axis=axis_num, keepdims=True)
    return centered * lax.rsqrt(variance + EPSILON) * gain


def per_device(pair_in, valid_tokens, proj_weight, out_weight, norm_gains):
    local_rows, count, width = pair_in.shape
    first_row = lax.axis_index("row") * local_rows
    valid = valid_tokens.astype(jnp.float32)
    own_valid = lax.dynamic_slice_in_dim(valid, first_row, local_rows, 0)
    mask = (own_valid[:, None] * valid[None, :]).reshape(local_rows * count)
    current = pair_in
    for update_index in range(2):
        incoming = update_index == 1
        proj = proj_weight[update_index]
        gains = norm_gains[update_index]
        normed = layer_norm(current.astype(jnp.float32), gains[0], 2).astype(jnp.bfloat16)
        flat_rows = normed.reshape(local_rows * count, width)
        projected = lax.dot_general(
            proj[:, 0 : 4 * width],
            flat_rows,
            (((0,), (1,)), ((), ())),
            preferred_element_type=jnp.float32,
        )
        gate_values = jax.nn.sigmoid(
            jnp.dot(flat_rows, proj[:, 4 * width :], preferred_element_type=jnp.float32)
        )
        edge_left = (
            jax.nn.sigmoid(projected[0:width]) * projected[width : 2 * width] * mask
        ).astype(jnp.bfloat16)
        edge_right = (
            jax.nn.sigmoid(projected[2 * width : 3 * width])
            * projected[3 * width : 4 * width]
            * mask
        ).astype(jnp.bfloat16)
        edge_left = edge_left.reshape(width, local_rows, count)
        edge_right = edge_right.reshape(width, local_rows, count)
        left_chan, right_chan = sent_together((edge_left, edge_right), "row", 0, 1, 2)
        if incoming:
            triangle = jnp.einsum(
                "cki,ckj->cij", left_chan, right_chan, preferred_element_type=jnp.float32
            )
        else:
            triangle = jnp.einsum(
                "cik,cjk->cij", left_chan, right_chan, preferred_element_type=jnp.float32
            )
        back_rows = lax.all_to_all(
            triangle.astype(jnp.bfloat16), "row", split_axis=1, concat_axis=0, tiled=True
        )
        output_normed = layer_norm(
            back_rows.astype(jnp.float32), gains[1][:, None, None], 0
        ).astype(jnp.bfloat16)
        update_rows = lax.dot_general(
            output_normed.reshape(width, local_rows * count),
            out_weight[update_index],
            (((0,), (0,)), ((), ())),
            preferred_element_type=jnp.float32,
        )
        update_rows = (update_rows * gate_values).reshape(local_rows, count, width)
        current = (current.astype(jnp.float32) + update_rows).astype(jnp.bfloat16)
    return current


def solution(mesh):
    return jax.shard_map(
        per_device,
        mesh=mesh,
        in_specs=(P(("groups", "row"), None, None), P("groups"), P(), P(), P()),
        out_specs=P(("groups", "row"), None, None),
        check_vma=False,
    )
```

profile of v0, /device:TPU:44, one launch (start us, length us, event | category | flops | bytes accessed | tf_op | source)
XLA Modules:
  0.0 713.2 jit_solution(5059751953196569143)
XLA Ops:
  0.0 0.8 convert_element_type.83
  1.0 0.8 slice_bitcast_fusion.2
  1.7 1.6 convert_reduce_fusion.1
  3.3 2.3 fusion.13
  5.7 1.3 fusion.15
  7.0 1.2 convolution_bitcast_fusion.1
  8.2 2.0 fusion.34
  10.2 2.7 copy.20
  12.9 1.7 copy.21
  14.6 1.8 pad_maximum_fusion
  16.4 233.1 %all_to_all.54 = bf16[128,8,1024]{2,1,0:T(8,128)(2,1)S(1)} all-to-all(bf16[128,8,1024]{2,1,0:T(8,128)(2,1)S(1)} %pad_maximum_fusion), channel_id=1, replica_groups=mesh['groups'=4,'row'=64] {'row'}, dimensions={0} | all-to-all | bytes 4194304 | tf_op jit(solution)/shard_map/all_to_all | solution.py:12
  249.5 0.2 copy.44
  249.7 0.7 convolution_convert_fusion.1
  250.4 2.0 copy.23
  252.5 6.7 all-to-all-start.1
  259.2 0.1 mul.180
  259.3 2.1 fusion.5
  261.4 106.9 %all-to-all-done.1 = bf16[2,512,512]{2,0,1:T(2,128)(2,1)S(1)} async-done(((bf16[2,512,512]{2,0,1:T(2,128)(2,1)}), bf16[2,512,512]{2,0,1:T(2,128)(2,1)S(1)}, u32[]{:S(2)}, u32[]{:S(2)}) %all-to-all-start.1) | async-done | bytes 1048608 | tf_op jit(solution)/shard_map/all_to_all | solution.py:64
  368.2 0.9 bitcast_convert_fusion.1
  369.1 0.3 bitcast_reduce_fusion.1
  369.4 0.4 multiply_reduce_fusion.1
  369.8 0.4 multiply_convert_fusion.1
  370.2 0.4 copy.33
  370.6 0.8 copy-done.1
  371.4 0.5 convolution_multiply_fusion.1
  371.9 0.6 convert_reduce_fusion
  372.6 1.3 fusion.10
  373.9 1.3 fusion.12
  375.1 1.2 convolution_bitcast_fusion
  376.4 2.0 fusion.24
  378.4 2.7 copy.25
  381.1 1.7 copy.26
  382.8 1.8 pad_maximum_fusion.1
  384.5 204.8 %all_to_all.55 = bf16[128,8,1024]{2,1,0:T(8,128)(2,1)S(1)} all-to-all(bf16[128,8,1024]{2,1,0:T(8,128)(2,1)S(1)} %pad_maximum_fusion.1), channel_id=1, replica_groups=mesh['groups'=4,'row'=64] {'row'}, dimensions={0} | all-to-all | bytes 4194304 | tf_op jit(solution)/shard_map/all_to_all | solution.py:12
  589.3 0.2 copy.43
  589.5 0.8 convolution_convert_fusion
  590.3 2.0 copy.29
  592.3 6.7 all-to-all-start.3
  599.2 2.1 fusion.2
  601.3 107.0 %all-to-all-done.3 = bf16[2,512,512]{2,0,1:T(2,128)(2,1)S(1)} async-done(((bf16[2,512,512]{2,0,1:T(2,128)(2,1)}), bf16[2,512,512]{2,0,1:T(2,128)(2,1)S(1)}, u32[]{:S(2)}, u32[]{:S(2)}) %all-to-all-start.3) | async-done | bytes 1048608 | tf_op jit(solution)/shard_map/all_to_all | solution.py:64
  708.3 0.9 bitcast_convert_fusion
  709.2 0.3 bitcast_reduce_fusion
  709.5 0.4 multiply_reduce_fusion
  709.9 0.4 multiply_convert_fusion
  710.3 0.4 copy.34
  710.7 0.8 copy-done.2
  711.5 0.5 convolution_multiply_fusion
  712.0 1.2 fusion.17
  (21 shorter events, 0.4 us)
Async XLA Ops:
  0.0 5.7 copy-start
  0.0 5.7 copy-start.3
  252.5 115.8 %all-to-all-start.1 = ((bf16[2,512,512]{2,0,1:T(2,128)(2,1)}), bf16[2,512,512]{2,0,1:T(2,128)(2,1)S(1)}, u32[]{:S(2)}, u32[]{:S(2)}) async-start(bf16[2,512,512]{2,0,1:T(2,128)(2,1)} %copy.23), calls=%async_computation.1 | async-start | bytes 2097152 | tf_op jit(solution)/shard_map/all_to_all | solution.py:64
  369.8 1.6 copy-start.1
  369.8 1.6 copy-start.4
  592.3 116.0 %all-to-all-start.3 = ((bf16[2,512,512]{2,0,1:T(2,128)(2,1)}), bf16[2,512,512]{2,0,1:T(2,128)(2,1)S(1)}, u32[]{:S(2)}, u32[]{:S(2)}) async-start(bf16[2,512,512]{2,0,1:T(2,128)(2,1)} %copy.29), calls=%async_computation.3 | async-start | bytes 2097152 | tf_op jit(solution)/shard_map/all_to_all | solution.py:64
  709.9 1.6 copy-start.2
where the time goes:
time: 714 us; the launch traced here: 713 us
  blocking collectives  438 us (61%)
  waiting for transfers between devices  214 us (30%)
  other arithmetic  21.9 us (3%)
  local copies, waits for them, and re-layouts  16.8 us (2%)
  starting transfers between devices  13.4 us (2%)
  matrix products  9.07 us (1%)
    all_to_all x2, blocking collectives, sent_together(): lax.all_to_all(both, axis, split_axis=split_dim, concat_axis=concat_dim,...  438 us
    all_to_all x2, waiting for transfers between devices, per_device(): lax.all_to_all(triangle.astype(jnp.bfloat16), 'row', split_axis=1, concat...  214 us
  transfers between devices with their start and end apart: 2, of which 2 were waited for; matrix products, arithmetic and copies ran while one was open for 1% of the time, Pallas kernels for 0%

commit v1 on v0

v1 whole, which is shorter than its diff:
```python
import functools

import jax
import jax.numpy as jnp
from jax import lax
from jax.experimental import pallas as pl
from jax.experimental.pallas import tpu as pltpu
from jax.sharding import PartitionSpec as P

MESH = pl.DeviceIdType.MESH
EPSILON = 1e-05
SPREAD = 7
LANES = 128
BF16 = jnp.bfloat16
F32 = jnp.float32


def dot(a, b, contract_a, contract_b):
    return lax.dot_general(
        a, b, (((contract_a,), (contract_b,)), ((), ())), preferred_element_type=F32
    )


def kernel(
    peers,
    pair_ref,
    mask_ref,
    wt_ref,
    wg_ref,
    wo_ref,
    gin_ref,
    gout_ref,
    out_ref,
    left_f,
    right_f,
    tri_f,
    normed,
    gates,
    middle,
    src0,
    src1,
    land_l0,
    land_r0,
    land_l1,
    land_r1,
    mat_l,
    mat_r,
    part,
    tri_out0,
    tri_out1,
    tri_in0,
    tri_in1,
    swap_out,
    swap_in,
    scat_send,
    scat_recv0,
    scat_recv1,
    swap_send,
    swap_recv,
    tri_send,
    tri_recv,
):
    rows, count, width = pair_ref.shape
    chips = peers // 2
    half = chips // 2
    inner = (SPREAD + 1) // 2
    outer = half - inner
    cols = count // 2
    blocks_per_half = cols // LANES
    me = lax.axis_index("row")
    chip = me // 2
    core = me % 2
    other = 1 - core

    def wrap(a):
        return lax.rem(a + 4 * chips, chips)

    def device(at_chip, at_core):
        return {"row": wrap(at_chip) * 2 + at_core}

    def send(src, dst, ssem, rsem, at_chip, at_core):
        pltpu.make_async_remote_copy(
            src_ref=src,
            dst_ref=dst,
            send_sem=ssem,
            recv_sem=rsem,
            device_id=device(at_chip, at_core),
            device_id_type=MESH,
        ).start()

    def waiter(ref, ssem, rsem):
        return pltpu.make_async_remote_copy(
            src_ref=ref,
            dst_ref=ref,
            send_sem=ssem,
            recv_sem=rsem,
            device_id=device(chip, other),
            device_id_type=MESH,
        )

    def role_of(chunk):
        return lax.rem(chip + chunk, 2)

    def owned_set(role):
        return wrap(chip - SPREAD * role)

    def base_of(role):
        return (chips - outer) + role * (inner - (chips - outer))

    def self_slot(role):
        return outer + role * (SPREAD - inner - outer)

    barrier = pltpu.get_barrier_semaphore()
    reach = 2 * outer + 1

    def greet(i, carry):
        at = chip - outer + i
        pl.semaphore_signal(
            barrier, inc=1, device_id=device(at, other), device_id_type=MESH
        )

        @pl.when(i != outer)
        def _():
            pl.semaphore_signal(
                barrier, inc=1, device_id=device(at, core), device_id_type=MESH
            )

        return carry

    lax.fori_loop(0, reach, greet, 0)

    def project(u, h, pair):
        span = pl.ds(h * cols, cols)

        def row(r, carry):
            z = pair[r, span, :].astype(F32)
            mean = jnp.mean(z, axis=1, keepdims=True)
            centered = z - mean
            var = jnp.mean(centered * centered, axis=1, keepdims=True)
            x = (centered * lax.rsqrt(var + EPSILON) * gin_ref[u]).astype(BF16)
            normed[r, span, :] = x
            m = mask_ref[pl.ds(r, 1), span]
            for k, store in ((2, right_f), (0, left_f)):
                gate = dot(wt_ref[u, k * width : (k + 1) * width, :], x, 1, 1)
                value = dot(wt_ref[u, (k + 1) * width : (k + 2) * width, :], x, 1, 1)
                edge = jax.nn.sigmoid(gate) * value * m
                for b in range(blocks_per_half):
                    store[h * blocks_per_half + b, pl.ds(r, width, stride=rows), :] = edge[
                        :, b * LANES : (b + 1) * LANES
                    ]
            return carry

        lax.fori_loop(0, rows, row, 0)

    def gate_values(u):
        def row(r, carry):
            gates[r] = jax.nn.sigmoid(dot(normed[r], wg_ref[u], 1, 0))
            return carry

        lax.fori_loop(0, rows, row, 0)

    tile = 2 * rows

    def packed(store, at, first, number):
        return jnp.concatenate(
            [store[first + b, at, :] for b in range(number)], axis=1
        ).astype(BF16)

    def finish(u, h, pair, result, tri_in):
        span = pl.ds(h * cols, cols)

        def unpack(p, carry):
            at = pl.ds(pl.multiple_of(p * tile, tile), tile)
            block = tri_in[h, p].astype(F32)
            for b in range(blocks_per_half):
                tri_f[b, at, :] = block[:, b * LANES : (b + 1) * LANES]
            return carry

        lax.fori_loop(0, peers, unpack, 0, unroll=4)

        def row(r, carry):
            t = jnp.concatenate(
                [tri_f[b, pl.ds(r, width, stride=rows), :] for b in range(blocks_per_half)], axis=1
            )
            mean = jnp.mean(t, axis=0, keepdims=True)
            centered = t - mean
            var = jnp.mean(centered * centered, axis=0, keepdims=True)
            y = (centered * lax.rsqrt(var + EPSILON) * gout_ref[u]).astype(BF16)
            update = dot(y, wo_ref[u], 0, 0)
            z = pair[r, span, :].astype(F32)
            result[r, span, :] = (z + update * gates[r, span, :]).astype(BF16)
            return carry

        lax.fori_loop(0, rows, row, 0)

    def scatter(chunk, items):
        odd = lax.rem(chip + chunk, 2)

        def step(k, carry):
            for role in range(2):
                if role == 0:
                    ahead = outer - odd - 2 * k
                    t = wrap(-ahead)
                    slot = odd + 2 * k
                else:
                    ahead = 2 * k - odd - (outer - 1)
                    t = SPREAD - ahead
                    slot = t - inner
                home = wrap(chip - t)
                for src, dst_of, ssem, rsem in items:
                    send(
                        src.at[home * 2 + other],
                        dst_of(role, slot * 2 + core),
                        ssem,
                        rsem(role),
                        chip + ahead,
                        other,
                    )

                    @pl.when(ahead != 0)
                    def _():
                        send(
                            src.at[home * 2 + core],
                            dst_of(role, slot * 2 + core),
                            ssem,
                            rsem(role),
                            chip + ahead,
                            core,
                        )

                    @pl.when(ahead == 0)
                    def _():
                        dst_of(role, slot * 2 + core)[...] = src[home * 2 + core]

            return carry

        lax.fori_loop(0, half // 2, step, 0)

    def return_tri(role, h, tri_out, tri_in, ssem, rsem):
        home = owned_set(role)
        base = base_of(role)
        own = self_slot(role)
        pair_index = home * 2 + core

        def step(i, carry):
            k = i + role * (half - 1 - 2 * i)
            at = home + base + k
            send(
                tri_out.at[role, h, 2 * k + other],
                tri_in.at[h, pair_index],
                ssem,
                rsem,
                at,
                other,
            )

            @pl.when(k != own)
            def _():
                send(
                    tri_out.at[role, h, 2 * k + core],
                    tri_in.at[h, pair_index],
                    ssem,
                    rsem,
                    at,
                    core,
                )

            @pl.when(k == own)
            def _():
                tri_in[h, pair_index] = tri_out[role, h, 2 * k + core]

            return carry

        lax.fori_loop(0, half, step, 0)

    for h in range(2):
        project(0, h, pair_ref)

    def pack0(p, carry):
        at = pl.ds(pl.multiple_of(p * tile, tile), tile)
        src0[0, p] = packed(right_f, at, 0, 2 * blocks_per_half)
        src0[1, p] = packed(left_f, at, 0, 2 * blocks_per_half)
        return carry

    lax.fori_loop(0, peers, pack0, 0, unroll=2)

    pl.semaphore_wait(barrier, 2 * reach - 1)

    def natural(role, slot_core):
        return land_r0.at[role, me]

    def slotted(role, slot_core):
        return land_l0.at[role, slot_core]

    for chunk in range(2):
        scatter(chunk, [(src0.at[0], natural, scat_send.at[0, chunk], lambda r: scat_recv0.at[0, r])])
        scatter(chunk, [(src0.at[1], slotted, scat_send.at[1, chunk], lambda r: scat_recv0.at[1, r])])

    gate_values(0)

    for chunk in range(2):
        role = role_of(chunk)
        home = owned_set(role)
        base = base_of(role)
        first = land_r0.at[role, pl.ds(0, peers // 2 - 1)]
        waiter(first, scat_send.at[0, 0], scat_recv0.at[0, role]).wait_recv()

        def pass_on(k, carry):
            at = wrap(home + base + k) * 2
            send(
                land_r0.at[role, pl.ds(at, 2)],
                land_r0.at[1 - role, pl.ds(at, 2)],
                swap_send.at[0, chunk],
                swap_recv.at[0, 1 - role],
                chip + SPREAD - 2 * SPREAD * role,
                core,
            )
            return carry

        lax.fori_loop(0, half, pass_on, 0)

    def multiply0(role):
        def split_r(s, carry):
            block = land_r0[role, pl.ds(2 * s, 2)].astype(F32)
            block = block.reshape(2, 2, rows, count)
            at = pl.ds(pl.multiple_of(s * tile, tile), tile)
            for e in range(2):
                mat_r[e, at, :] = block[:, e].reshape(tile, count).astype(BF16)
            return carry

        lax.fori_loop(0, chips, split_r, 0)

        def split_l(s, carry):
            block = land_l0[role, pl.ds(2 * s, 2)].astype(F32)
            block = block.reshape(2, 2, rows, count)
            at = pl.ds(pl.multiple_of(s * tile, tile), tile)
            for e in range(2):
                mat_l[e, at, :] = block[:, e].reshape(tile, count).astype(BF16)
            return carry

        lax.fori_loop(0, half, split_l, 0)
        for h in range(2):
            blocks = []
            for e in range(2):
                product = dot(
                    mat_l[e, 0 : half * tile, :], mat_r[e, h * cols : (h + 1) * cols, :], 1, 1
                )
                blocks.append(product.reshape(peers // 2, 1, rows, cols))
            both = jnp.concatenate(blocks, axis=1).reshape(peers // 2, tile, cols)
            tri_out0[role, h] = both.astype(BF16)

    def ready0(chunk):
        role = role_of(chunk)
        waiter(
            land_l0.at[role, pl.ds(0, peers // 2 - 1)], scat_send.at[1, 0], scat_recv0.at[1, role]
        ).wait_recv()
        waiter(
            land_r0.at[role, pl.ds(0, peers // 2)], swap_send.at[0, 0], swap_recv.at[0, role]
        ).wait_recv()
        multiply0(role)

    def give0(chunk, h):
        return_tri(role_of(chunk), h, tri_out0, tri_in0, tri_send.at[0, chunk, h], tri_recv.at[0, h])

    ready0(0)
    give0(0, 0)
    ready0(1)
    give0(1, 0)
    give0(0, 1)
    give0(1, 1)

    def arrived(u, h, tri_in):
        waiter(
            tri_in.at[h, pl.ds(0, peers - 2)], tri_send.at[u, 0, h], tri_recv.at[u, h]
        ).wait_recv()

    for h in range(2):
        arrived(0, h, tri_in0)
        finish(0, h, pair_ref, middle, tri_in0)
        project(1, h, middle)

        def pack1(p, carry):
            at = pl.ds(pl.multiple_of(p * tile, tile), tile)
            src1[h, 0, p] = packed(right_f, at, h * blocks_per_half, blocks_per_half)
            src1[h, 1, p] = packed(left_f, at, h * blocks_per_half, blocks_per_half)
            return carry

        lax.fori_loop(0, peers, pack1, 0, unroll=2)
        for chunk in range(2):
            scatter(
                chunk,
                [
                    (
                        src1.at[h, 0],
                        lambda role, s, h=h: land_r1.at[role, h, s],
                        scat_send.at[2 + 2 * h, chunk],
                        lambda r, h=h: scat_recv1.at[0, h, r],
                    ),
                    (
                        src1.at[h, 1],
                        lambda role, s, h=h: land_l1.at[role, h, s],
                        scat_send.at[3 + 2 * h, chunk],
                        lambda r, h=h: scat_recv1.at[1, h, r],
                    ),
                ],
            )

    gate_values(1)

    def multiply1(role):
        def split(s, carry):
            at = pl.ds(pl.multiple_of(s * tile, tile), tile)
            for land, mat in ((land_l1, mat_l), (land_r1, mat_r)):
                for h in range(2):
                    block = land[role, h, pl.ds(2 * s, 2)].astype(F32)
                    block = block.reshape(2, 2, rows, cols)
                    for e in range(2):
                        mat[e, at, h * cols : (h + 1) * cols] = (
                            block[:, e].reshape(tile, cols).astype(BF16)
                        )
            return carry

        lax.fori_loop(0, half, split, 0)
        depth = half * tile
        for e in range(2):
            for b in range(2):
                a = mat_l[e, 0:depth, b * cols : (b + 1) * cols]
                product = dot(a, mat_r[e, 0:depth, :], 0, 0)
                part[role, b * (peers // 2) : (b + 1) * (peers // 2), e * rows : (e + 1) * rows, :] = (
                    product.reshape(peers // 2, rows, count)
                )

    for chunk in range(2):
        role = role_of(chunk)
        home = owned_set(role)
        for kind, land in ((0, land_r1), (1, land_l1)):
            for h in range(2):
                waiter(
                    land.at[role, h, pl.ds(0, peers // 2 - 1)],
                    scat_send.at[2, 0],
                    scat_recv1.at[kind, h, role],
                ).wait_recv()
        multiply1(role)
        far = base_of(1 - role)

        def round_far(k, carry):
            at = wrap(home + far + k) * 2
            swap_out[role, pl.ds(2 * k, 2)] = part[role, pl.ds(at, 2)].astype(BF16)
            return carry

        lax.fori_loop(0, half, round_far, 0)
        send(
            swap_out.at[role],
            swap_in.at[1 - role],
            swap_send.at[1, chunk],
            swap_recv.at[1, 1 - role],
            chip + SPREAD - 2 * SPREAD * role,
            core,
        )

    def ready1(chunk):
        role = role_of(chunk)
        home = owned_set(role)
        near = base_of(role)
        waiter(swap_in.at[role], swap_send.at[1, 0], swap_recv.at[1, role]).wait_recv()

        def total(k, carry):
            at = wrap(home + near + k) * 2
            both = part[role, pl.ds(at, 2)] + swap_in[role, pl.ds(2 * k, 2)].astype(F32)
            both = both.astype(BF16)
            for h in range(2):
                tri_out1[role, h, pl.ds(2 * k, 2)] = both[:, :, h * cols : (h + 1) * cols]
            return carry

        lax.fori_loop(0, half, total, 0)

    def give1(chunk, h):
        return_tri(role_of(chunk), h, tri_out1, tri_in1, tri_send.at[1, chunk, h], tri_recv.at[1, h])

    ready1(0)
    give1(0, 0)
    ready1(1)
    give1(1, 0)
    give1(0, 1)
    give1(1, 1)

    for h in range(2):
        arrived(1, h, tri_in1)
        finish(1, h, middle, out_ref, tri_in1)

    sent = peers // 2 - 1
    for chunk in range(2):
        for kind in range(2):
            waiter(
                src0.at[kind, pl.ds(0, sent)], scat_send.at[kind, chunk], scat_recv0.at[0, 0]
            ).wait_send()
            for h in range(2):
                waiter(
                    src1.at[h, kind, pl.ds(0, sent)],
                    scat_send.at[2 + 2 * h + kind, chunk],
                    scat_recv0.at[0, 0],
                ).wait_send()
        waiter(
            land_r0.at[0, pl.ds(0, peers // 2)], swap_send.at[0, chunk], swap_recv.at[0, 0]
        ).wait_send()
        waiter(swap_out.at[0], swap_send.at[1, chunk], swap_recv.at[1, 0]).wait_send()
        for h in range(2):
            waiter(
                tri_out0.at[0, h, pl.ds(0, sent)], tri_send.at[0, chunk, h], tri_recv.at[0, h]
            ).wait_send()
            waiter(
                tri_out1.at[0, h, pl.ds(0, sent)], tri_send.at[1, chunk, h], tri_recv.at[1, h]
            ).wait_send()


def per_device(peers, pair_in, valid_tokens, proj_weight, out_weight, norm_gains):
    rows, count, width = pair_in.shape
    cols = count // 2
    tile = 2 * rows
    first_row = lax.axis_index("row") * rows
    valid = valid_tokens.astype(F32)
    mask = lax.dynamic_slice_in_dim(valid, first_row, rows, 0)[:, None] * valid[None, :]
    weight_t = jnp.transpose(proj_weight[:, :, : 4 * width], (0, 2, 1))
    weight_g = proj_weight[:, :, 4 * width :]
    gain_in = norm_gains[:, 0:1, :]
    gain_out = norm_gains[:, 1, :, None]
    vmem = pltpu.VMEM
    dma = pltpu.SemaphoreType.DMA
    near = peers // 2
    block = pl.BlockSpec(memory_space=pltpu.VMEM)
    return pl.pallas_call(
        functools.partial(kernel, peers),
        out_shape=jax.ShapeDtypeStruct((rows, count, width), BF16),
        in_specs=[block] * 7,
        out_specs=block,
        scratch_shapes=[
            vmem((count // LANES, width * rows, LANES), F32),
            vmem((count // LANES, width * rows, LANES), F32),
            vmem((cols // LANES, width * rows, LANES), F32),
            vmem((rows, count, width), BF16),
            vmem((rows, count, width), F32),
            vmem((rows, count, width), BF16),
            vmem((2, peers, tile, count), BF16),
            vmem((2, 2, peers, tile, cols), BF16),
            vmem((2, near, tile, count), BF16),
            vmem((2, peers, tile, count), BF16),
            vmem((2, 2, near, tile, cols), BF16),
            vmem((2, 2, near, tile, cols), BF16),
            vmem((2, count, count), BF16),
            vmem((2, count, count), BF16),
            vmem((2, peers, tile, count), F32),
            vmem((2, 2, near, tile, cols), BF16),
            vmem((2, 2, near, tile, cols), BF16),
            vmem((2, peers, tile, cols), BF16),
            vmem((2, peers, tile, cols), BF16),
            vmem((2, near, tile, count), BF16),
            vmem((2, near, tile, count), BF16),
            dma((6, 2)),
            dma((2, 2)),
            dma((2, 2, 2)),
            dma((2, 2)),
            dma((2, 2)),
            dma((2, 2, 2)),
            dma((2, 2)),
        ],
        compiler_params=pltpu.CompilerParams(
            collective_id=0, has_side_effects=True, vmem_limit_bytes=60 * 1024 * 1024
        ),
    )(pair_in, mask, weight_t, weight_g, out_weight, gain_in, gain_out)


def solution(mesh):
    return jax.shard_map(
        functools.partial(per_device, mesh.shape["row"]),
        mesh=mesh,
        in_specs=(P(("groups", "row"), None, None), P("groups"), P(), P(), P()),
        out_specs=P(("groups", "row"), None, None),
        check_vma=False,
    )
```

time: 714 us -> 565 us (0.79)
  Pallas kernels: 0 us -> 556 us
  blocking collectives: 438 us -> 0 us
  waiting for transfers between devices: 214 us -> 0 us
  other arithmetic: 21.9 us -> 0.67 us
  starting transfers between devices: 13.4 us -> 0 us
  matrix products: 9.07 us -> 0 us
  local copies, waits for them, and re-layouts: 16.8 us -> 8.26 us
    pallas_call x0 -> x1, Pallas kernels: none -> 556 us  [per_device(): pl.pallas_call(functools.partial(kernel, peers), out_shape=jax.ShapeDtype...]
    all_to_all x2 -> x0, blocking collectives: 438 us -> none  [sent_together(): lax.all_to_all(both, axis, split_axis=split_dim, concat_axis=concat_dim,...]
    all_to_all x2 -> x0, waiting for transfers between devices: 214 us -> none  [per_device(): lax.all_to_all(triangle.astype(jnp.bfloat16), 'row', split_axis=1, concat...]
    all_to_all x2 -> x0, starting transfers between devices: 13.4 us -> none  [per_device(): lax.all_to_all(triangle.astype(jnp.bfloat16), 'row', split_axis=1, concat...]
    convert_element_type x10 -> x1, other arithmetic: 11 us -> 0.01 us  [per_device(): valid = valid_tokens.astype(F32)]
    dot_general x8 -> x0, matrix products: 9.07 us -> none  [the longest x2 4.12 us: per_device(): jnp.dot(flat_rows, proj[:, 4 * width:], preferred_element_type=jnp.float32)]
    reshape x4 -> x0, local copies, waits for them, and re-layouts: 8.74 us -> none  [the longest x2 5.4 us: per_device(): edge_left = edge_left.reshape(width, local_rows, count)]
    reduce_sum x8 -> x0, other arithmetic: 7.21 us -> none  [the longest x4 4.36 us: layer_norm(): variance = jnp.mean(centered * centered, axis=axis_num, keepdims=True)]
  transfers between devices with their start and end apart: 2 -> 0, of which waited for: 2 -> 0; matrix products, arithmetic and copies ran while one was open for 1% -> 0% of each run, Pallas kernels for 0% -> 0%
where the time goes in v1:
time: 565 us; the launch traced here: 564 us
  Pallas kernels  556 us (98%)
  local copies, waits for them, and re-layouts  8.26 us (1%)
    pallas_call x1, Pallas kernels, per_device(): pl.pallas_call(functools.partial(kernel, peers), out_shape=jax.ShapeDtype...  556 us

profile of v1, /device:TPU:44, one launch (start us, length us, event | category | flops | bytes accessed | tf_op | source)
XLA Modules:
  0.0 564.4 jit_solution(6489204368265910796)
XLA Ops:
  0.0 0.0 copy-start
  0.0 0.7 copy-done
  0.7 0.0 copy-start.1
  0.7 0.1 dynamic_slice.3
  0.8 0.6 copy-done.1
  1.4 0.6 fusion
  1.9 0.7 broadcast_multiply_fusion.mask_ref
  2.6 1.5 slice.13.wg_ref
  4.1 0.8 copy.9.gout_ref
  4.9 0.0 slice-start
  4.9 0.9 slice-done
  5.8 0.8 copy.10
  6.7 555.5 %shard_map.55 = bf16[8,512,128]{2,1,0:T(8,128)(2,1)} custom-call(bf16[8,512,128]{2,1,0:T(8,128)(2,1)} %pair_ref.1, f32[8,512]{1,0:T(8,128)} %broadcast_multiply_fusion.mask_ref, bf16[2,512,128]{2,1,0:T(8,128)(2,1)} %bitcast.2, bf16[2,128,128]{2,1,0:T(8,128)(2,1)} %slice.13.wg_ref, bf16[2,128,128]{2,1,0:T(8,128)(2,1)} %wo_ref.1, ...), custom_call_target="tpu_custom_call" | custom-call | tf_op jit(solution)/shard_map/pallas_call | solution.py:531
  562.2 2.3 copy.12
  (1 shorter events, 0.0 us)
Async XLA Ops:
  0.0 0.7 copy-start
  0.7 0.7 copy-start.1
  4.9 0.9 slice-start

commit v2 on v1

v2 whole, which is shorter than its diff:
```python
import functools

import jax
import jax.numpy as jnp
from jax import lax
from jax.experimental import pallas as pl
from jax.experimental.pallas import tpu as pltpu
from jax.sharding import PartitionSpec as P

MESH = pl.DeviceIdType.MESH
EPSILON = 1e-05
OWNERS = 4
STEP = 3
LANES = 128
BF16 = jnp.bfloat16
F32 = jnp.float32


def dot(a, b, contract_a, contract_b):
    return lax.dot_general(
        a, b, (((contract_a,), (contract_b,)), ((), ())), preferred_element_type=F32
    )


class Plan:
    def __init__(self, peers):
        self.chips = peers // 2
        self.span = (OWNERS - 1) * STEP
        self.outer = (self.chips - self.span - 1) // 2
        self.inner = (STEP - 1) // 2
        edge = self.outer + self.inner + 1
        self.starts = [0] + [edge + STEP * k for k in range(OWNERS - 1)] + [self.chips]
        self.edge = edge
        self.flow = self.chips - edge
        self.deep = 16


def kernel(
    peers,
    pair_ref,
    valid_ref,
    valid_s,
    proj_ref,
    wo_ref,
    gain_ref,
    out_ref,
    wt,
    gain_col,
    left_f,
    right_f,
    tri_f,
    normed,
    gates,
    middle,
    src0,
    src1,
    land_l0,
    land_r0,
    land_l1,
    land_r1,
    mat_l,
    mat_r,
    tri_s,
    part,
    tri_out0,
    tri_out1,
    tri_in0,
    tri_in1,
    flow_out,
    flow_in,
    scat_send,
    scat_recv0,
    scat_recv1,
    relay_send,
    relay_recv,
    flow_send,
    flow_recv,
    tri_send,
    tri_recv,
):
    rows, count, width = pair_ref.shape
    plan = Plan(peers)
    chips, outer, span, starts = plan.chips, plan.outer, plan.span, plan.starts
    cols = count // 2
    blocks_per_half = cols // LANES
    tile = 2 * rows
    me = lax.axis_index("row")
    chip = me // 2
    core = me % 2
    other = 1 - core

    def wrap(a):
        return lax.rem(a + 4 * chips, chips)

    def device(at_chip, at_core):
        return {"row": wrap(at_chip) * 2 + at_core}

    def send(src, dst, ssem, rsem, at_chip, at_core):
        pltpu.make_async_remote_copy(
            src_ref=src,
            dst_ref=dst,
            send_sem=ssem,
            recv_sem=rsem,
            device_id=device(at_chip, at_core),
            device_id_type=MESH,
        ).start()

    def waiter(ref, ssem, rsem):
        return pltpu.make_async_remote_copy(
            src_ref=ref,
            dst_ref=ref,
            send_sem=ssem,
            recv_sem=rsem,
            device_id=device(chip, other),
            device_id_type=MESH,
        )

    def length(role):
        return starts[role + 1] - starts[role]

    def remote(role):
        return 2 * length(role) - 1

    def own_slot(role):
        return outer + STEP * role

    def parity(chunk):
        return lax.rem(chip + chunk, 2)

    def each(chunk, action):
        for role in range(OWNERS):
            pl.when(parity(chunk) == role % 2)(functools.partial(action, role))

    def start_of(role):
        return (plan.edge - STEP + STEP * role) * ((role + OWNERS - 1) // OWNERS)

    def length_of(role):
        end = (2 * role - (OWNERS - 1)) * (2 * role - (OWNERS - 1)) // ((OWNERS - 1) * (OWNERS - 1))
        return STEP + (plan.edge - STEP) * end

    barrier = pltpu.get_barrier_semaphore()
    reach = 2 * outer + 1

    def greet(i, carry):
        at = chip - outer + i
        pl.semaphore_signal(
            barrier, inc=1, device_id=device(at, other), device_id_type=MESH
        )

        @pl.when(i != outer)
        def _():
            pl.semaphore_signal(
                barrier, inc=1, device_id=device(at, core), device_id_type=MESH
            )

        return carry

    lax.fori_loop(0, reach, greet, 0)

    for u in range(2):
        for k in range(4):
            at = slice(k * width, (k + 1) * width)
            wt[u, at, :] = jnp.transpose(proj_ref[u, :, at].astype(F32)).astype(BF16)
        gain_col[u] = jnp.transpose(jnp.broadcast_to(gain_ref[u, 1:2, :], (width, width)))

    def project(u, h, pair):
        there = pl.ds(h * cols, cols)
        valid = valid_ref[:, h * cols : (h + 1) * cols].astype(F32)

        def row(r, carry):
            z = pair[r, there, :].astype(F32)
            mean = jnp.mean(z, axis=1, keepdims=True)
            centered = z - mean
            var = jnp.mean(centered * centered, axis=1, keepdims=True)
            x = (centered * lax.rsqrt(var + EPSILON) * gain_ref[u, 0:1, :]).astype(BF16)
            normed[r, there, :] = x
            m = valid * valid_s[me * rows + r].astype(F32)
            for k, store in ((2, right_f), (0, left_f)):
                gate = dot(wt[u, k * width : (k + 1) * width, :], x, 1, 1)
                value = dot(wt[u, (k + 1) * width : (k + 2) * width, :], x, 1, 1)
                edge = jax.nn.sigmoid(gate) * value * m
                for b in range(blocks_per_half):
                    store[h * blocks_per_half + b, pl.ds(r, width, stride=rows), :] = edge[
                        :, b * LANES : (b + 1) * LANES
                    ]
            return carry

        lax.fori_loop(0, rows, row, 0)

    def gate_values(u):
        def row(r, carry):
            gates[r] = jax.nn.sigmoid(dot(normed[r], proj_ref[u, :, 4 * width :], 1, 0))
            return carry

        lax.fori_loop(0, rows, row, 0)

    def packed(store, at, first, number):
        return jnp.concatenate(
            [store[first + b, at, :] for b in range(number)], axis=1
        ).astype(BF16)

    def finish(u, h, pair, result, tri_in):
        there = pl.ds(h * cols, cols)

        def unpack(p, carry):
            at = pl.ds(pl.multiple_of(p * tile, tile), tile)
            block = tri_in[h, p].astype(F32)
            for b in range(blocks_per_half):
                tri_f[b, at, :] = block[:, b * LANES : (b + 1) * LANES]
            return carry

        lax.fori_loop(0, peers, unpack, 0, unroll=4)

        def row(r, carry):
            t = jnp.concatenate(
                [tri_f[b, pl.ds(r, width, stride=rows), :] for b in range(blocks_per_half)], axis=1
            )
            mean = jnp.mean(t, axis=0, keepdims=True)
            centered = t - mean
            var = jnp.mean(centered * centered, axis=0, keepdims=True)
            scaled = centered * lax.rsqrt(var + EPSILON)
            gain = jnp.concatenate([gain_col[u]] * blocks_per_half, axis=1)
            update = dot((scaled * gain).astype(BF16), wo_ref[u], 0, 0)
            z = pair[r, there, :].astype(F32)
            result[r, there, :] = (z + update * gates[r, there, :]).astype(BF16)
            return carry

        lax.fori_loop(0, rows, row, 0)

    def scatter(chunk, items):
        odd = parity(chunk)

        def step_to(t, role):
            ahead = STEP * role - t
            home = wrap(chip - t)
            slot = t + outer
            for src, dst_of, ssem, rsem in items:
                send(
                    src.at[home * 2 + other],
                    dst_of(role, slot * 2 + core),
                    ssem,
                    rsem(role),
                    chip + ahead,
                    other,
                )

                @pl.when(ahead != 0)
                def _():
                    send(
                        src.at[home * 2 + core],
                        dst_of(role, slot * 2 + core),
                        ssem,
                        rsem(role),
                        chip + ahead,
                        core,
                    )

                @pl.when(ahead == 0)
                def _():
                    dst_of(role, slot * 2 + core)[...] = src[home * 2 + core]

        def outside(k, carry):
            step_to(1 - outer - odd + 2 * k, 0)
            step_to(span + outer - odd - 2 * k, OWNERS - 1)
            return carry

        lax.fori_loop(0, (outer + 1) // 2, outside, 0)

        def inside(k, carry):
            t = 2 - odd + 2 * k
            step_to(t, (t + plan.inner) // STEP)
            return carry

        lax.fori_loop(0, chips // 2 - (outer + 1), inside, 0)

    def return_tri(role, h, tri_out, tri_in, ssem, rsem):
        home = wrap(chip - STEP * role)
        last = starts[role + 1] - 1

        def step(i, carry):
            slot = starts[role] + i if 2 * role < OWNERS else last - i
            at = home - outer + slot
            send(
                tri_out.at[h, slot * 2 + other], tri_in.at[h, home * 2 + core], ssem, rsem, at, other
            )

            @pl.when(slot != own_slot(role))
            def _():
                send(
                    tri_out.at[h, slot * 2 + core],
                    tri_in.at[h, home * 2 + core],
                    ssem,
                    rsem,
                    at,
                    core,
                )

            @pl.when(slot == own_slot(role))
            def _():
                tri_in[h, home * 2 + core] = tri_out[h, slot * 2 + core]

            return carry

        lax.fori_loop(0, length(role), step, 0)

    for h in range(2):
        project(0, h, pair_ref)

    def pack0(p, carry):
        at = pl.ds(pl.multiple_of(p * tile, tile), tile)
        src0[0, p] = packed(right_f, at, 0, 2 * blocks_per_half)
        src0[1, p] = packed(left_f, at, 0, 2 * blocks_per_half)
        return carry

    lax.fori_loop(0, peers, pack0, 0, unroll=2)

    pl.semaphore_wait(barrier, 2 * reach - 1)

    for chunk in range(2):
        scatter(
            chunk,
            [
                (
                    src0.at[0],
                    lambda role, s: land_r0.at[role, s],
                    scat_send.at[0, chunk],
                    lambda r: scat_recv0.at[0, r],
                )
            ],
        )
        scatter(
            chunk,
            [
                (
                    src0.at[1],
                    lambda role, s: land_l0.at[s],
                    scat_send.at[1, chunk],
                    lambda r: scat_recv0.at[1, r],
                )
            ],
        )

    gate_values(0)

    def pieces(role, piece):
        return pl.ds(2 * starts[piece], 2 * length(piece))

    def relay(role, piece, way):
        to = role + way
        if 0 <= to < OWNERS:
            send(
                land_r0.at[role, pieces(role, piece)],
                land_r0.at[to, pieces(role, piece)],
                relay_send.at[role, piece, (way + 1) // 2],
                relay_recv.at[to, piece],
                chip + STEP * way,
                core,
            )

    def relay_own(role):
        ref = land_r0.at[role, pl.ds(0, remote(role))]
        waiter(ref, scat_send.at[0, 0], scat_recv0.at[0, role]).wait_recv()
        relay(role, role, 1)
        relay(role, role, -1)

    def relay_more(gap, role):
        for way in (1, -1):
            piece = role - way * gap
            if 0 <= piece < OWNERS:
                ref = land_r0.at[role, pieces(role, piece)]
                waiter(ref, scat_send.at[0, 0], relay_recv.at[role, piece]).wait_recv()
                relay(role, piece, way)

    for chunk in range(2):
        each(chunk, relay_own)
    for gap in range(1, OWNERS):
        for chunk in range(2):
            each(chunk, functools.partial(relay_more, gap))

    most = plan.edge
    mat_l[...] = jnp.zeros_like(mat_l)
    mat_r[...] = jnp.zeros_like(mat_r)

    def multiply0(role):
        home = wrap(chip - STEP * role)
        start = start_of(role)

        def split_r(s, carry):
            block = land_r0[role, pl.ds(2 * s, 2)].astype(F32)
            block = block.reshape(2, 2, rows, count)
            at = pl.ds(pl.multiple_of(wrap(home - outer + s) * tile, tile), tile)
            for e in range(2):
                mat_r[e, at, :] = block[:, e].reshape(tile, count).astype(BF16)
            return carry

        lax.fori_loop(0, chips, split_r, 0)

        def split_l(s, carry):
            block = land_l0[pl.ds(2 * (start + s), 2)].astype(F32)
            block = block.reshape(2, 2, rows, count)
            at = pl.ds(pl.multiple_of(s * tile, tile), tile)
            for e in range(2):
                mat_l[e, at, :] = block[:, e].reshape(tile, count).astype(BF16)
            return carry

        lax.fori_loop(0, length_of(role), split_l, 0)
        for h in range(2):
            blocks = []
            for e in range(2):
                product = dot(
                    mat_l[e, 0 : most * tile, :], mat_r[e, h * cols : (h + 1) * cols, :], 1, 1
                )
                blocks.append(product.reshape(2 * most, 1, rows, cols))
            both = jnp.concatenate(blocks, axis=1).reshape(2 * most, tile, cols)
            tri_s[h] = both.astype(BF16)

        def keep(s, carry):
            for h in range(2):
                tri_out0[h, pl.ds(2 * (start + s), 2)] = tri_s[h, pl.ds(2 * s, 2)]
            return carry

        lax.fori_loop(0, length_of(role), keep, 0)

    def ready0(chunk):
        def wait_left(role):
            ref = land_l0.at[pl.ds(0, remote(role))]
            waiter(ref, scat_send.at[1, 0], scat_recv0.at[1, role]).wait_recv()

        each(chunk, wait_left)

        def one(i, carry):
            multiply0(parity(chunk) + 2 * i)
            return carry

        lax.fori_loop(0, OWNERS // 2, one, 0)

    def give(u, chunk, h, tri_out, tri_in):
        def one(role):
            return_tri(role, h, tri_out, tri_in, tri_send.at[u, role, h], tri_recv.at[u, h])

        each(chunk, one)

    ready0(0)
    give(0, 0, 0, tri_out0, tri_in0)
    ready0(1)
    give(0, 1, 0, tri_out0, tri_in0)
    give(0, 0, 1, tri_out0, tri_in0)
    give(0, 1, 1, tri_out0, tri_in0)

    def arrived(u, h, tri_in):
        waiter(
            tri_in.at[h, pl.ds(0, peers - OWNERS)], tri_send.at[u, 0, h], tri_recv.at[u, h]
        ).wait_recv()

    for h in range(2):
        arrived(0, h, tri_in0)
        finish(0, h, pair_ref, middle, tri_in0)
        project(1, h, middle)

        def pack1(p, carry):
            at = pl.ds(pl.multiple_of(p * tile, tile), tile)
            src1[h, 0, p] = packed(right_f, at, h * blocks_per_half, blocks_per_half)
            src1[h, 1, p] = packed(left_f, at, h * blocks_per_half, blocks_per_half)
            return carry

        lax.fori_loop(0, peers, pack1, 0, unroll=2)
        for chunk in range(2):
            scatter(
                chunk,
                [
                    (
                        src1.at[h, 0],
                        lambda role, s, h=h: land_r1.at[h, s],
                        scat_send.at[2 + 2 * h, chunk],
                        lambda r, h=h: scat_recv1.at[0, h, r],
                    ),
                    (
                        src1.at[h, 1],
                        lambda role, s, h=h: land_l1.at[h, s],
                        scat_send.at[3 + 2 * h, chunk],
                        lambda r, h=h: scat_recv1.at[1, h, r],
                    ),
                ],
            )

    gate_values(1)

    def multiply1(role):
        start = start_of(role)
        used = length_of(role)

        def split(s, carry):
            at = pl.ds(pl.multiple_of(s * tile, tile), tile)

            @pl.when(s < used)
            def _():
                for land, mat in ((land_l1, mat_l), (land_r1, mat_r)):
                    for h in range(2):
                        block = land[h, pl.ds(2 * (start + s), 2)].astype(F32)
                        block = block.reshape(2, 2, rows, cols)
                        for e in range(2):
                            mat[e, at, h * cols : (h + 1) * cols] = (
                                block[:, e].reshape(tile, cols).astype(BF16)
                            )

            @pl.when(s >= used)
            def _():
                for mat in (mat_l, mat_r):
                    for e in range(2):
                        mat[e, at, :] = jnp.zeros((tile, count), BF16)

            return carry

        lax.fori_loop(0, plan.deep, split, 0)
        depth = plan.deep * tile
        for e in range(2):
            for b in range(2):
                a = mat_l[e, 0:depth, b * cols : (b + 1) * cols]
                product = dot(a, mat_r[e, 0:depth, :], 0, 0)
                part[role, b * (peers // 2) : (b + 1) * (peers // 2), e * rows : (e + 1) * rows, :] = (
                    product.reshape(peers // 2, rows, count)
                )

    flow = plan.flow

    def passing(role, way):
        if way > 0:
            return starts[role + 1], chips, chips - flow, role
        return 0, starts[role], 0, OWNERS - 1 - role

    def flow_on(role, way):
        low, high, first, index = passing(role, way)
        home = wrap(chip - STEP * role)
        side = (way + 1) // 2
        joined = 0 <= role - way < OWNERS
        if joined:
            wait_flow(role, way)

        def step(i, carry):
            slot = low + i
            at = wrap(home - outer + slot) * 2
            there = pl.ds(2 * (slot - first), 2)
            value = part[role, pl.ds(at, 2)]
            if joined:
                value = value + flow_in[side, index - 1, there].astype(F32)
            flow_out[side, index, there] = value.astype(BF16)
            return carry

        lax.fori_loop(0, high - low, step, 0)
        there = pl.ds(2 * (low - first), 2 * (high - low))
        send(
            flow_out.at[side, index, there],
            flow_in.at[side, index, there],
            flow_send.at[side, index],
            flow_recv.at[side, index],
            chip + STEP * way,
            core,
        )

    def wait_flow(role, way):
        low, high, first, index = passing(role - way, way)
        side = (way + 1) // 2
        there = pl.ds(2 * (low - first), 2 * (high - low))
        waiter(
            flow_in.at[side, index, there], flow_send.at[side, index], flow_recv.at[side, index]
        ).wait_recv()

    def begin1(role):
        for kind, land in ((0, land_r1), (1, land_l1)):
            for h in range(2):
                waiter(
                    land.at[h, pl.ds(0, remote(role))], scat_send.at[2, 0], scat_recv1.at[kind, h, role]
                ).wait_recv()

    def flow_stage(stage, role):
        for way in (1, -1):
            source = 0 if way > 0 else OWNERS - 1
            if role == source + way * stage and 0 <= role + way < OWNERS:
                flow_on(role, way)

    for chunk in range(2):
        each(chunk, begin1)

        def one(i, carry):
            multiply1(parity(chunk) + 2 * i)
            return carry

        lax.fori_loop(0, OWNERS // 2, one, 0)
        each(chunk, functools.partial(flow_stage, 0))
    for stage in range(1, OWNERS - 1):
        for chunk in range(2):
            each(chunk, functools.partial(flow_stage, stage))

    def ready1(chunk):
        def one(role):
            home = wrap(chip - STEP * role)
            ends = []
            if role == OWNERS - 1:
                wait_flow(role, 1)
            if role == 0:
                wait_flow(role, -1)
            for way in (1, -1):
                if 0 <= role - way < OWNERS:
                    _, _, first, index = passing(role - way, way)
                    ends.append(((way + 1) // 2, index, first))

            def total(i, carry):
                slot = starts[role] + i
                at = wrap(home - outer + slot) * 2
                value = part[role, pl.ds(at, 2)]
                for side, index, first in ends:
                    value = value + flow_in[side, index, pl.ds(2 * (slot - first), 2)].astype(F32)
                value = value.astype(BF16)
                for h in range(2):
                    tri_out1[h, pl.ds(2 * slot, 2)] = value[:, :, h * cols : (h + 1) * cols]
                return carry

            lax.fori_loop(0, length(role), total, 0)

        each(chunk, one)

    ready1(0)
    give(1, 0, 0, tri_out1, tri_in1)
    ready1(1)
    give(1, 1, 0, tri_out1, tri_in1)
    give(1, 0, 1, tri_out1, tri_in1)
    give(1, 1, 1, tri_out1, tri_in1)

    for h in range(2):
        arrived(1, h, tri_in1)
        finish(1, h, middle, out_ref, tri_in1)

    sent = peers // 2 - OWNERS // 2
    for chunk in range(2):
        for kind in range(2):
            waiter(
                src0.at[kind, pl.ds(0, sent)], scat_send.at[kind, chunk], scat_recv0.at[0, 0]
            ).wait_send()
            for h in range(2):
                waiter(
                    src1.at[h, kind, pl.ds(0, sent)],
                    scat_send.at[2 + 2 * h + kind, chunk],
                    scat_recv0.at[0, 0],
                ).wait_send()
    for role in range(OWNERS):
        for way in (1, -1):
            side = (way + 1) // 2
            if 0 <= role + way < OWNERS:
                low, high, first, index = passing(role, way)
                there = pl.ds(2 * (low - first), 2 * (high - low))
                waiter(
                    flow_out.at[side, index, there], flow_send.at[side, index], flow_recv.at[0, 0]
                ).wait_send()
                for piece in range(OWNERS):
                    if piece == role or (piece < role) == (way > 0):
                        waiter(
                            land_r0.at[role, pieces(role, piece)],
                            relay_send.at[role, piece, side],
                            relay_recv.at[0, 0],
                        ).wait_send()
        for h in range(2):
            for u, tri_out in ((0, tri_out0), (1, tri_out1)):
                waiter(
                    tri_out.at[h, pl.ds(0, remote(role))], tri_send.at[u, role, h], tri_recv.at[u, h]
                ).wait_send()


def per_device(peers, pair_in, valid_tokens, proj_weight, out_weight, norm_gains):
    rows, count, width = pair_in.shape
    cols = count // 2
    tile = 2 * rows
    plan = Plan(peers)
    vmem = pltpu.VMEM
    dma = pltpu.SemaphoreType.DMA
    near = peers // 2
    block = pl.BlockSpec(memory_space=pltpu.VMEM)
    return pl.pallas_call(
        functools.partial(kernel, peers),
        out_shape=jax.ShapeDtypeStruct((rows, count, width), BF16),
        in_specs=[block, block, pl.BlockSpec(memory_space=pltpu.SMEM), block, block, block],
        out_specs=block,
        scratch_shapes=[
            vmem((2, 4 * width, width), BF16),
            vmem((2, width, width), F32),
            vmem((count // LANES, width * rows, LANES), F32),
            vmem((count // LANES, width * rows, LANES), F32),
            vmem((cols // LANES, width * rows, LANES), F32),
            vmem((rows, count, width), BF16),
            vmem((rows, count, width), F32),
            vmem((rows, count, width), BF16),
            vmem((2, peers, tile, count), BF16),
            vmem((2, 2, peers, tile, cols), BF16),
            vmem((peers, tile, count), BF16),
            vmem((OWNERS, peers, tile, count), BF16),
            vmem((2, peers, tile, cols), BF16),
            vmem((2, peers, tile, cols), BF16),
            vmem((2, plan.deep * tile, count), BF16),
            vmem((2, count, count), BF16),
            vmem((2, 2 * plan.edge, tile, cols), BF16),
            vmem((OWNERS, peers, tile, count), F32),
            vmem((2, peers, tile, cols), BF16),
            vmem((2, peers, tile, cols), BF16),
            vmem((2, peers, tile, cols), BF16),
            vmem((2, peers, tile, cols), BF16),
            vmem((2, OWNERS - 1, 2 * plan.flow, tile, count), BF16),
            vmem((2, OWNERS - 1, 2 * plan.flow, tile, count), BF16),
            dma((6, 2)),
            dma((2, OWNERS)),
            dma((2, 2, OWNERS)),
            dma((OWNERS, OWNERS, 2)),
            dma((OWNERS, OWNERS)),
            dma((2, OWNERS - 1)),
            dma((2, OWNERS - 1)),
            dma((2, OWNERS, 2)),
            dma((2, 2)),
        ],
        compiler_params=pltpu.CompilerParams(
            collective_id=0, has_side_effects=True, vmem_limit_bytes=62 * 1024 * 1024
        ),
    )(pair_in, valid_tokens.reshape(1, count), valid_tokens, proj_weight, out_weight, norm_gains)


def solution(mesh):
    return jax.shard_map(
        functools.partial(per_device, mesh.shape["row"]),
        mesh=mesh,
        in_specs=(P(("groups", "row"), None, None), P("groups"), P(), P(), P()),
        out_specs=P(("groups", "row"), None, None),
        check_vma=False,
    )
```

time: 565 us -> 565 us (level)
  Pallas kernels: 556 us -> 563 us
  local copies, waits for them, and re-layouts: 8.26 us -> 2.27 us
    pallas_call x1, Pallas kernels: 556 us -> 563 us  [per_device(): pl.pallas_call(functools.partial(kernel, peers), out_shape=jax.ShapeDtype...]
where the time goes in v2:
time: 565 us
  Pallas kernels  563 us (100%)
    pallas_call x1, Pallas kernels, per_device(): pl.pallas_call(functools.partial(kernel, peers), out_shape=jax.ShapeDtype...  563 us

profile of v2, /device:TPU:44, one launch (start us, length us, event | category | flops | bytes accessed | tf_op | source)
XLA Modules:
  0.0 565.2 jit_solution(14780399072818860560)
XLA Ops:
  0.0 562.9 %shard_map.55 = bf16[8,512,128]{2,1,0:T(8,128)(2,1)} custom-call(bf16[8,512,128]{2,1,0:T(8,128)(2,1)} %pair_ref.1, s32[1,512]{1,0:T(1,128)} %bitcast.1, s32[512]{0:T(512)} %valid_s.1, bf16[2,128,640]{2,1,0:T(8,128)(2,1)} %proj_ref.1, bf16[2,128,128]{2,1,0:T(8,128)(2,1)} %wo_ref.1, f32[2,2,128]{2,1,0:T(2,128)} %gain_ref.1), custom_call_target="tpu_custom_call" | custom-call | tf_op jit(solution)/shard_map/pallas_call | solution.py:677
  562.9 2.3 copy.7

commit v3 on v2

v3 whole, which is shorter than its diff:
```python
import functools

import jax
import jax.numpy as jnp
from jax import lax
from jax.experimental import pallas as pl
from jax.experimental.pallas import tpu as pltpu
from jax.sharding import PartitionSpec as P

MESH = pl.DeviceIdType.MESH
EPSILON = 1e-05
OWNERS = 4
STEP = 3
LANES = 128
BF16 = jnp.bfloat16
F32 = jnp.float32


def dot(a, b, contract_a, contract_b):
    return lax.dot_general(
        a, b, (((contract_a,), (contract_b,)), ((), ())), preferred_element_type=F32
    )


class Plan:
    def __init__(self, peers):
        self.chips = peers // 2
        self.span = (OWNERS - 1) * STEP
        self.outer = (self.chips - self.span - 1) // 2
        self.inner = (STEP - 1) // 2
        edge = self.outer + self.inner + 1
        self.starts = [0] + [edge + STEP * k for k in range(OWNERS - 1)] + [self.chips]
        self.edge = edge
        self.flow = self.chips - edge
        self.deep = 16


def kernel(
    peers,
    pair_ref,
    valid_ref,
    valid_s,
    proj_ref,
    wo_ref,
    gain_ref,
    out_ref,
    wt,
    gain_col,
    left_f,
    right_f,
    tri_f,
    normed,
    gates,
    middle,
    src0,
    src1,
    land_l0,
    land_r0,
    land1,
    mat_l,
    mat_r,
    tri_s,
    part,
    tri_out0,
    tri_out1,
    tri_in0,
    tri_in1,
    flow_out,
    flow_in,
    scat_send,
    scat_recv0,
    scat_recv1,
    relay_send,
    relay_recv,
    flow_send,
    flow_recv,
    tri_send,
    tri_recv,
):
    rows, count, width = pair_ref.shape
    plan = Plan(peers)
    chips, outer, span, starts = plan.chips, plan.outer, plan.span, plan.starts
    cols = count // 2
    blocks_per_half = cols // LANES
    tile = 2 * rows
    me = lax.axis_index("row")
    chip = me // 2
    core = me % 2
    other = 1 - core

    def wrap(a):
        return lax.rem(a + 4 * chips, chips)

    def device(at_chip, at_core):
        return {"row": wrap(at_chip) * 2 + at_core}

    def send(src, dst, ssem, rsem, at_chip, at_core):
        pltpu.make_async_remote_copy(
            src_ref=src,
            dst_ref=dst,
            send_sem=ssem,
            recv_sem=rsem,
            device_id=device(at_chip, at_core),
            device_id_type=MESH,
        ).start()

    def waiter(ref, ssem, rsem):
        return pltpu.make_async_remote_copy(
            src_ref=ref,
            dst_ref=ref,
            send_sem=ssem,
            recv_sem=rsem,
            device_id=device(chip, other),
            device_id_type=MESH,
        )

    def length(role):
        return starts[role + 1] - starts[role]

    def remote(role):
        return 2 * length(role) - 1

    def start_of(role):
        return (plan.edge - STEP + STEP * role) * ((role + OWNERS - 1) // OWNERS)

    def length_of(role):
        end = (2 * role - (OWNERS - 1)) * (2 * role - (OWNERS - 1)) // ((OWNERS - 1) * (OWNERS - 1))
        return STEP + (plan.edge - STEP) * end

    barrier = pltpu.get_barrier_semaphore()
    reach = 2 * outer + 1

    def greet(i, carry):
        at = chip - outer + i
        pl.semaphore_signal(
            barrier, inc=1, device_id=device(at, other), device_id_type=MESH
        )

        @pl.when(i != outer)
        def _():
            pl.semaphore_signal(
                barrier, inc=1, device_id=device(at, core), device_id_type=MESH
            )

        return carry

    lax.fori_loop(0, reach, greet, 0)

    for u in range(2):
        for k in range(4):
            at = slice(k * width, (k + 1) * width)
            wt[u, at, :] = jnp.transpose(proj_ref[u, :, at].astype(F32)).astype(BF16)
        gain_col[u] = jnp.transpose(jnp.broadcast_to(gain_ref[u, 1:2, :], (width, width)))

    def project(u, h, pair):
        there = pl.ds(h * cols, cols)
        valid = valid_ref[:, h * cols : (h + 1) * cols].astype(F32)

        def row(r, carry):
            z = pair[r, there, :].astype(F32)
            mean = jnp.mean(z, axis=1, keepdims=True)
            centered = z - mean
            var = jnp.mean(centered * centered, axis=1, keepdims=True)
            x = (centered * lax.rsqrt(var + EPSILON) * gain_ref[u, 0:1, :]).astype(BF16)
            normed[r, there, :] = x
            m = valid * valid_s[me * rows + r].astype(F32)
            for k, store in ((2, right_f), (0, left_f)):
                gate = dot(wt[u, k * width : (k + 1) * width, :], x, 1, 1)
                value = dot(wt[u, (k + 1) * width : (k + 2) * width, :], x, 1, 1)
                edge = jax.nn.sigmoid(gate) * value * m
                for b in range(blocks_per_half):
                    store[h * blocks_per_half + b, pl.ds(r, width, stride=rows), :] = edge[
                        :, b * LANES : (b + 1) * LANES
                    ]
            return carry

        lax.fori_loop(0, rows, row, 0)

    def gate_values(u):
        def row(r, carry):
            gates[r] = jax.nn.sigmoid(dot(normed[r], proj_ref[u, :, 4 * width :], 1, 0))
            return carry

        lax.fori_loop(0, rows, row, 0)

    def packed(store, p, e, first, number):
        at = pl.ds(pl.multiple_of(p * tile + e * rows, rows), rows)
        return jnp.concatenate(
            [store[first + b, at, :] for b in range(number)], axis=1
        ).astype(BF16)

    def finish(u, h, pair, result, tri_in):
        there = pl.ds(h * cols, cols)

        def unpack(p, carry):
            for e in range(2):
                at = pl.ds(pl.multiple_of(p * tile + e * rows, rows), rows)
                block = tri_in[h, e, p].astype(F32)
                for b in range(blocks_per_half):
                    tri_f[b, at, :] = block[:, b * LANES : (b + 1) * LANES]
            return carry

        lax.fori_loop(0, peers, unpack, 0, unroll=4)

        def row(r, carry):
            t = jnp.concatenate(
                [tri_f[b, pl.ds(r, width, stride=rows), :] for b in range(blocks_per_half)], axis=1
            )
            mean = jnp.mean(t, axis=0, keepdims=True)
            centered = t - mean
            var = jnp.mean(centered * centered, axis=0, keepdims=True)
            scaled = centered * lax.rsqrt(var + EPSILON)
            gain = jnp.concatenate([gain_col[u]] * blocks_per_half, axis=1)
            update = dot((scaled * gain).astype(BF16), wo_ref[u], 0, 0)
            z = pair[r, there, :].astype(F32)
            result[r, there, :] = (z + update * gates[r, there, :]).astype(BF16)
            return carry

        lax.fori_loop(0, rows, row, 0)

    def scatter(src, dst_of, ssem, rsem):
        def step_to(t, role, owned):
            ahead = STEP * role - t
            home = wrap(chip - t)
            dst = dst_of(role, (t + outer) * 2 + core)
            send(src.at[home * 2 + other], dst, ssem, rsem(role), chip + ahead, other)

            def remote_copy():
                send(src.at[home * 2 + core], dst, ssem, rsem(role), chip + ahead, core)

            if not owned:
                remote_copy()
                return
            pl.when(ahead != 0)(remote_copy)

            @pl.when(ahead == 0)
            def _():
                dst[...] = src[home * 2 + core]

        def outside(k, carry):
            step_to(k - outer, 0, False)
            step_to(span + outer - k, OWNERS - 1, False)
            return carry

        lax.fori_loop(0, outer, outside, 0)

        def inside(t, carry):
            step_to(t, (t + plan.inner) // STEP, True)
            return carry

        lax.fori_loop(0, span + 1, inside, 0)

    def return_tri(u, e, h, tri_out, tri_in):
        ssem = tri_send.at[u, e, h]
        rsem = tri_recv.at[u, e, h]

        def step_to(role, slot, own):
            home = wrap(chip - STEP * role)
            at = home - outer + slot
            dst = tri_in.at[h, e, home * 2 + core]
            send(tri_out.at[h, e, slot * 2 + other], dst, ssem, rsem, at, other)

            @pl.when(jnp.logical_not(own))
            def _():
                send(tri_out.at[h, e, slot * 2 + core], dst, ssem, rsem, at, core)

            @pl.when(own)
            def _():
                dst[...] = tri_out[h, e, slot * 2 + core]

        def ends(i, carry):
            step_to(0, i, i == outer)
            step_to(OWNERS - 1, chips - 1 - i, i == outer)
            return carry

        lax.fori_loop(0, plan.edge, ends, 0)

        def between(i, carry):
            for role in range(1, OWNERS - 1):
                step_to(role, starts[role] + i, i == plan.inner)
            return carry

        lax.fori_loop(0, STEP, between, 0)

    for h in range(2):
        project(0, h, pair_ref)

    def pack0(p, carry):
        for e in range(2):
            src0[0, e, p] = packed(right_f, p, e, 0, 2 * blocks_per_half)
            src0[1, e, p] = packed(left_f, p, e, 0, 2 * blocks_per_half)
        return carry

    lax.fori_loop(0, peers, pack0, 0, unroll=2)

    pl.semaphore_wait(barrier, 2 * reach - 1)

    def scatter_right(e):
        scatter(
            src0.at[0, e],
            lambda role, s: land_r0.at[e, role, s],
            scat_send.at[0, e],
            lambda role: scat_recv0.at[0, e, role],
        )

    def scatter_left(e):
        scatter(
            src0.at[1, e],
            lambda role, s: land_l0.at[e, s],
            scat_send.at[1, e],
            lambda role: scat_recv0.at[1, e, role],
        )

    def pieces(piece):
        return pl.ds(2 * starts[piece], 2 * length(piece))

    def relay(e, role, piece, way):
        to = role + way
        if 0 <= to < OWNERS:
            send(
                land_r0.at[e, role, pieces(piece)],
                land_r0.at[e, to, pieces(piece)],
                relay_send.at[e, role, piece, (way + 1) // 2],
                relay_recv.at[e, to, piece],
                chip + STEP * way,
                core,
            )

    def relay_own(e):
        for role in (0, OWNERS - 1, *range(1, OWNERS - 1)):
            ref = land_r0.at[e, role, pl.ds(0, remote(role))]
            waiter(ref, scat_send.at[0, 0], scat_recv0.at[0, e, role]).wait_recv()
            relay(e, role, role, 1)
            relay(e, role, role, -1)

    def relay_more(e, gap):
        for role in range(OWNERS):
            for way in (1, -1):
                piece = role - way * gap
                if 0 <= piece < OWNERS:
                    ref = land_r0.at[e, role, pieces(piece)]
                    waiter(ref, scat_send.at[0, 0], relay_recv.at[e, role, piece]).wait_recv()
                    relay(e, role, piece, way)

    most = plan.edge
    mat_l[...] = jnp.zeros_like(mat_l)
    mat_r[...] = jnp.zeros_like(mat_r)

    def multiply0(e, role):
        home = wrap(chip - STEP * role)
        start = start_of(role)

        def split_r(s, carry):
            block = land_r0[e, role, pl.ds(2 * s, 2)].astype(F32).reshape(tile, count)
            at = pl.ds(pl.multiple_of(wrap(home - outer + s) * tile, tile), tile)
            mat_r[at, :] = block.astype(BF16)
            return carry

        lax.fori_loop(0, chips, split_r, 0)

        def split_l(s, carry):
            block = land_l0[e, pl.ds(2 * (start + s), 2)].astype(F32).reshape(tile, count)
            at = pl.ds(pl.multiple_of(s * tile, tile), tile)
            mat_l[at, :] = block.astype(BF16)
            return carry

        lax.fori_loop(0, length_of(role), split_l, 0)
        for h in range(2):
            product = dot(mat_l[0 : most * tile, :], mat_r[h * cols : (h + 1) * cols, :], 1, 1)
            tri_s[h] = product.reshape(2 * most, rows, cols).astype(BF16)

        def keep(s, carry):
            for h in range(2):
                tri_out0[h, e, pl.ds(2 * (start + s), 2)] = tri_s[h, pl.ds(2 * s, 2)]
            return carry

        lax.fori_loop(0, length_of(role), keep, 0)

    def multiply_all(multiply, e):
        def one(role, carry):
            multiply(e, role)
            return carry

        lax.fori_loop(0, OWNERS, one, 0)

    def ready0(e):
        for role in range(OWNERS):
            ref = land_l0.at[e, pl.ds(0, remote(role))]
            waiter(ref, scat_send.at[1, 0], scat_recv0.at[1, e, role]).wait_recv()
        multiply_all(multiply0, e)

    scatter_right(0)
    scatter_right(1)
    gate_values(0)
    relay_own(0)
    scatter_left(0)
    relay_own(1)
    relay_more(0, 1)
    scatter_left(1)
    relay_more(1, 1)
    for gap in range(2, OWNERS - 1):
        relay_more(0, gap)
        relay_more(1, gap)
    relay_more(0, OWNERS - 1)
    ready0(0)
    return_tri(0, 0, 0, tri_out0, tri_in0)
    relay_more(1, OWNERS - 1)
    ready0(1)
    return_tri(0, 1, 0, tri_out0, tri_in0)
    return_tri(0, 0, 1, tri_out0, tri_in0)
    return_tri(0, 1, 1, tri_out0, tri_in0)

    def arrived(u, h, tri_in):
        for e in range(2):
            waiter(
                tri_in.at[h, e, pl.ds(0, peers - OWNERS)], tri_send.at[u, 0, h], tri_recv.at[u, e, h]
            ).wait_recv()

    for h in range(2):
        arrived(0, h, tri_in0)
        finish(0, h, pair_ref, middle, tri_in0)
        project(1, h, middle)

        def pack1(p, carry):
            for e in range(2):
                for kind, store in ((0, right_f), (1, left_f)):
                    src1[h, e, p, kind] = packed(store, p, e, h * blocks_per_half, blocks_per_half)
            return carry

        lax.fori_loop(0, peers, pack1, 0, unroll=2)
        for e in range(2):
            scatter(
                src1.at[h, e],
                lambda role, s, h=h, e=e: land1.at[h, e, s],
                scat_send.at[2 + h, e],
                lambda role, h=h, e=e: scat_recv1.at[h, e, role],
            )

    gate_values(1)

    def multiply1(e, role):
        start = start_of(role)
        used = length_of(role)

        def split(s, carry):
            at = pl.ds(pl.multiple_of(s * tile, tile), tile)

            @pl.when(s < used)
            def _():
                for kind, mat in ((1, mat_l), (0, mat_r)):
                    for h in range(2):
                        block = land1[h, e, pl.ds(2 * (start + s), 2), kind].astype(F32)
                        mat[at, h * cols : (h + 1) * cols] = block.reshape(tile, cols).astype(BF16)

            @pl.when(s >= used)
            def _():
                for mat in (mat_l, mat_r):
                    mat[at, :] = jnp.zeros((tile, count), BF16)

            return carry

        lax.fori_loop(0, plan.deep, split, 0)
        depth = plan.deep * tile
        for b in range(2):
            a = mat_l[0:depth, b * cols : (b + 1) * cols]
            product = dot(a, mat_r[0:depth, :], 0, 0)
            part[e, role, b * (peers // 2) : (b + 1) * (peers // 2)] = product.reshape(
                peers // 2, rows, count
            )

    flow = plan.flow

    def passing(role, way):
        if way > 0:
            return starts[role + 1], chips, chips - flow, role
        return 0, starts[role], 0, OWNERS - 1 - role

    def flow_on(e, role, way):
        low, high, first, index = passing(role, way)
        home = wrap(chip - STEP * role)
        side = (way + 1) // 2
        joined = 0 <= role - way < OWNERS
        if joined:
            wait_flow(e, role, way)

        def step(i, carry):
            slot = low + i
            at = wrap(home - outer + slot) * 2
            there = pl.ds(2 * (slot - first), 2)
            value = part[e, role, pl.ds(at, 2)]
            if joined:
                value = value + flow_in[e, side, index - 1, there].astype(F32)
            flow_out[e, side, index, there] = value.astype(BF16)
            return carry

        lax.fori_loop(0, high - low, step, 0)
        there = pl.ds(2 * (low - first), 2 * (high - low))
        send(
            flow_out.at[e, side, index, there],
            flow_in.at[e, side, index, there],
            flow_send.at[e, side, index],
            flow_recv.at[e, side, index],
            chip + STEP * way,
            core,
        )

    def wait_flow(e, role, way):
        low, high, first, index = passing(role - way, way)
        side = (way + 1) // 2
        there = pl.ds(2 * (low - first), 2 * (high - low))
        waiter(
            flow_in.at[e, side, index, there],
            flow_send.at[e, side, index],
            flow_recv.at[e, side, index],
        ).wait_recv()

    def begin1(e):
        for role in range(OWNERS):
            for h in range(2):
                ref = land1.at[h, e, pl.ds(0, remote(role))]
                waiter(ref, scat_send.at[2, 0], scat_recv1.at[h, e, role]).wait_recv()
        multiply_all(multiply1, e)

    def flow_stage(e, stage):
        flow_on(e, stage, 1)
        flow_on(e, OWNERS - 1 - stage, -1)

    for e in range(2):
        begin1(e)
        flow_stage(e, 0)
    for stage in range(1, OWNERS - 1):
        for e in range(2):
            flow_stage(e, stage)

    def ready1(e):
        wait_flow(e, OWNERS - 1, 1)
        wait_flow(e, 0, -1)
        for role in range(OWNERS):
            home = wrap(chip - STEP * role)
            ends = []
            for way in (1, -1):
                if 0 <= role - way < OWNERS:
                    _, _, first, index = passing(role - way, way)
                    ends.append(((way + 1) // 2, index, first))

            def total(i, carry):
                slot = starts[role] + i
                at = wrap(home - outer + slot) * 2
                value = part[e, role, pl.ds(at, 2)]
                for side, index, first in ends:
                    there = pl.ds(2 * (slot - first), 2)
                    value = value + flow_in[e, side, index, there].astype(F32)
                value = value.astype(BF16)
                for h in range(2):
                    tri_out1[h, e, pl.ds(2 * slot, 2)] = value[:, :, h * cols : (h + 1) * cols]
                return carry

            lax.fori_loop(0, length(role), total, 0)

    ready1(0)
    return_tri(1, 0, 0, tri_out1, tri_in1)
    ready1(1)
    return_tri(1, 1, 0, tri_out1, tri_in1)
    return_tri(1, 0, 1, tri_out1, tri_in1)
    return_tri(1, 1, 1, tri_out1, tri_in1)

    for h in range(2):
        arrived(1, h, tri_in1)
        finish(1, h, middle, out_ref, tri_in1)

    sent = peers - OWNERS
    for e in range(2):
        for kind in range(2):
            waiter(
                src0.at[kind, e, pl.ds(0, sent)], scat_send.at[kind, e], scat_recv0.at[0, 0, 0]
            ).wait_send()
        for h in range(2):
            waiter(
                src1.at[h, e, pl.ds(0, sent)], scat_send.at[2 + h, e], scat_recv0.at[0, 0, 0]
            ).wait_send()
            for u, tri_out in ((0, tri_out0), (1, tri_out1)):
                waiter(
                    tri_out.at[h, e, pl.ds(0, sent)], tri_send.at[u, e, h], tri_recv.at[u, e, h]
                ).wait_send()
        for role in range(OWNERS):
            for way in (1, -1):
                side = (way + 1) // 2
                if 0 <= role + way < OWNERS:
                    low, high, first, index = passing(role, way)
                    there = pl.ds(2 * (low - first), 2 * (high - low))
                    waiter(
                        flow_out.at[e, side, index, there],
                        flow_send.at[e, side, index],
                        flow_recv.at[0, 0, 0],
                    ).wait_send()
                    for piece in range(OWNERS):
                        if piece == role or (piece < role) == (way > 0):
                            waiter(
                                land_r0.at[e, role, pieces(piece)],
                                relay_send.at[e, role, piece, side],
                                relay_recv.at[0, 0, 0],
                            ).wait_send()


def per_device(peers, pair_in, valid_tokens, proj_weight, out_weight, norm_gains):
    rows, count, width = pair_in.shape
    cols = count // 2
    tile = 2 * rows
    plan = Plan(peers)
    vmem = pltpu.VMEM
    dma = pltpu.SemaphoreType.DMA
    block = pl.BlockSpec(memory_space=pltpu.VMEM)
    return pl.pallas_call(
        functools.partial(kernel, peers),
        out_shape=jax.ShapeDtypeStruct((rows, count, width), BF16),
        in_specs=[block, block, pl.BlockSpec(memory_space=pltpu.SMEM), block, block, block],
        out_specs=block,
        scratch_shapes=[
            vmem((2, 4 * width, width), BF16),
            vmem((2, width, width), F32),
            vmem((count // LANES, width * rows, LANES), F32),
            vmem((count // LANES, width * rows, LANES), F32),
            vmem((cols // LANES, width * rows, LANES), F32),
            vmem((rows, count, width), BF16),
            vmem((rows, count, width), F32),
            vmem((rows, count, width), BF16),
            vmem((2, 2, peers, rows, count), BF16),
            vmem((2, 2, peers, 2, rows, cols), BF16),
            vmem((2, peers, rows, count), BF16),
            vmem((2, OWNERS, peers, rows, count), BF16),
            vmem((2, 2, peers, 2, rows, cols), BF16),
            vmem((plan.deep * tile, count), BF16),
            vmem((count, count), BF16),
            vmem((2, 2 * plan.edge, rows, cols), BF16),
            vmem((2, OWNERS, peers, rows, count), F32),
            vmem((2, 2, peers, rows, cols), BF16),
            vmem((2, 2, peers, rows, cols), BF16),
            vmem((2, 2, peers, rows, cols), BF16),
            vmem((2, 2, peers, rows, cols), BF16),
            vmem((2, 2, OWNERS - 1, 2 * plan.flow, rows, count), BF16),
            vmem((2, 2, OWNERS - 1, 2 * plan.flow, rows, count), BF16),
            dma((4, 2)),
            dma((2, 2, OWNERS)),
            dma((2, 2, OWNERS)),
            dma((2, OWNERS, OWNERS, 2)),
            dma((2, OWNERS, OWNERS)),
            dma((2, 2, OWNERS - 1)),
            dma((2, 2, OWNERS - 1)),
            dma((2, 2, 2)),
            dma((2, 2, 2)),
        ],
        compiler_params=pltpu.CompilerParams(
            collective_id=0, has_side_effects=True, vmem_limit_bytes=62 * 1024 * 1024
        ),
    )(pair_in, valid_tokens.reshape(1, count), valid_tokens, proj_weight, out_weight, norm_gains)


def solution(mesh):
    return jax.shard_map(
        functools.partial(per_device, mesh.shape["row"]),
        mesh=mesh,
        in_specs=(P(("groups", "row"), None, None), P("groups"), P(), P(), P()),
        out_specs=P(("groups", "row"), None, None),
        check_vma=False,
    )
```

time: 565 us -> 535 us (0.947)
  Pallas kernels: 563 us -> 532 us
    pallas_call x1, Pallas kernels: 563 us -> 532 us  [per_device(): pl.pallas_call(functools.partial(kernel, peers), out_shape=jax.ShapeDtype...]
where the time goes in v3:
time: 535 us; the launch traced here: 534 us
  Pallas kernels  532 us (99%)
    pallas_call x1, Pallas kernels, per_device(): pl.pallas_call(functools.partial(kernel, peers), out_shape=jax.ShapeDtype...  532 us

profile of v3, /device:TPU:44, one launch (start us, length us, event | category | flops | bytes accessed | tf_op | source)
XLA Modules:
  0.0 534.3 jit_solution(3742829616014948234)
XLA Ops:
  0.0 532.0 %shard_map.55 = bf16[8,512,128]{2,1,0:T(8,128)(2,1)} custom-call(bf16[8,512,128]{2,1,0:T(8,128)(2,1)} %pair_ref.1, s32[1,512]{1,0:T(1,128)} %bitcast.1, s32[512]{0:T(512)} %valid_s.1, bf16[2,128,640]{2,1,0:T(8,128)(2,1)} %proj_ref.1, bf16[2,128,128]{2,1,0:T(8,128)(2,1)} %wo_ref.1, f32[2,2,128]{2,1,0:T(2,128)} %gain_ref.1), custom_call_target="tpu_custom_call" | custom-call | tf_op jit(solution)/shard_map/pallas_call | solution.py:613
  532.0 2.3 copy.7

commit v4 on v0

v4 whole, which is shorter than its diff:
```python
import functools

import jax
import jax.numpy as jnp
from jax import lax
from jax.experimental import pallas as pl
from jax.experimental.pallas import tpu as pltpu
from jax.sharding import PartitionSpec as P

MESH = pl.DeviceIdType.MESH
EPSILON = 1e-05
COLUMNS = 4
PARTS = 4
LANES = 128
BF16 = jnp.bfloat16
F32 = jnp.float32


def dot(a, b, contract_a, contract_b):
    return lax.dot_general(
        a, b, (((contract_a,), (contract_b,)), ((), ())), preferred_element_type=F32
    )


def kernel(
    peers,
    across,
    pair_ref,
    valid_ref,
    proj_ref,
    wo_ref,
    gain_ref,
    out_ref,
    wt,
    gain_col,
    left_f,
    right_f,
    tri_f,
    normed,
    gates,
    valid_own,
    valid_got,
    start_z,
    middle,
    final_z,
    home_z,
    relay_in,
    relay_out,
    src,
    land,
    mat_l,
    mat_r,
    tri_out,
    tri_in,
    valid_send,
    valid_recv,
    in_send,
    in_recv,
    in_relay_send,
    in_relay_recv,
    out_send,
    out_recv,
    out_relay_send,
    out_relay_recv,
    scat_send,
    scat_recv,
    tri_send,
    tri_recv,
):
    rows, count, width = pair_ref.shape
    chips = peers // 2
    length = chips // COLUMNS
    side = length // 2
    outer = (chips - length) // 2
    cols = count // 2
    part_cols = count // PARTS
    blocks_per_half = cols // LANES
    tile = 2 * rows
    me = lax.axis_index("row")
    chip = me // 2
    core = me % 2
    other = 1 - core
    group = lax.axis_index("groups")
    down = (group // across) % 2
    right = (group % across) % 2
    column = 2 * down + right
    block = chip // length
    offset = chip % length

    def device(at_column, at_chip, at_core):
        at_group = group + (at_column // 2 - down) * across + (at_column % 2 - right)
        return {"groups": at_group, "row": at_chip * 2 + at_core}

    def copier(from_ref, to_ref, ssem, rsem, at):
        return pltpu.make_async_remote_copy(
            src_ref=from_ref,
            dst_ref=to_ref,
            send_sem=ssem,
            recv_sem=rsem,
            device_id=at,
            device_id_type=MESH,
        )

    def send(from_ref, to_ref, ssem, rsem, at):
        copier(from_ref, to_ref, ssem, rsem, at).start()

    def waiter(ref, ssem, rsem):
        return copier(ref, ref, ssem, rsem, device(column, chip, other))

    def mirror(half, value):
        return value + half * (length - 1 - 2 * value)

    def placed(at_chip, of_group):
        t = (at_chip - length * of_group + outer + chips) % chips - outer
        half = (t + outer) // (2 * length)
        a = mirror(half, t) + outer
        at_column = a % COLUMNS
        w = (at_column + 1 + a // COLUMNS) % COLUMNS
        return at_column, length * of_group + mirror(half, w)

    def origin(at_column, at_offset):
        half = at_offset // side
        w = mirror(half, at_offset)
        k = (w - at_column - 1 + 2 * COLUMNS) % COLUMNS
        t = mirror(half, COLUMNS * k + at_column - outer)
        return (length * block + t + chips) % chips

    to_column, to_chip = placed(chip, column)
    from_chip = origin(column, offset)
    mine = from_chip * 2 + core
    owner = (offset * COLUMNS + column) * 2 + core
    stays = jnp.logical_and(to_column == column, to_chip == chip)
    moves = jnp.logical_not(stays)

    barrier = pltpu.get_barrier_semaphore()

    def greet_block(k, carry):
        at_chip = length * block + (offset + k) % length
        for i in range(COLUMNS):
            at_column = (column + i) % COLUMNS
            at = device(at_column, at_chip, other)
            pl.semaphore_signal(barrier, inc=1, device_id=at, device_id_type=MESH)
            at = device(at_column, at_chip, core)
            if i == 0:

                @pl.when(k != 0)
                def _():
                    pl.semaphore_signal(barrier, inc=1, device_id=at, device_id_type=MESH)
            else:
                pl.semaphore_signal(barrier, inc=1, device_id=at, device_id_type=MESH)
        return carry

    lax.fori_loop(0, length, greet_block, 0)

    def greet_column(k, carry):
        at = device(column, (length * (block + 1) + k) % chips, core)
        pl.semaphore_signal(barrier, inc=1, device_id=at, device_id_type=MESH)
        return carry

    lax.fori_loop(0, chips - length, greet_column, 0)

    valid_own[...] = jnp.broadcast_to(valid_ref[...].astype(F32), valid_own.shape)

    for u in range(2):
        for k in range(4):
            at = slice(k * width, (k + 1) * width)
            wt[u, at, :] = jnp.transpose(proj_ref[u, :, at].astype(F32)).astype(BF16)
        gain_col[u] = jnp.transpose(jnp.broadcast_to(gain_ref[u, 1:2, :], (width, width)))

    pl.semaphore_wait(barrier, 2 * COLUMNS * length - 1 + chips - length)

    def part(ref, f):
        return ref.at[:, pl.ds(f * part_cols, part_cols), :]

    two_steps = jnp.logical_and(to_column != column, to_chip != chip)
    one_step = jnp.logical_and(moves, jnp.logical_not(two_steps))

    @pl.when(block == column)
    def _():
        for i in range(1, COLUMNS):
            at = device((column + i) % COLUMNS, chip, core)
            send(valid_own, valid_got, valid_send.at[i - 1], valid_recv, at)
        valid_got[...] = valid_own[...]

    for f in range(PARTS):

        @pl.when(two_steps)
        def _():
            at = device(to_column, chip, core)
            dst = relay_in.at[column, :, pl.ds(f * part_cols, part_cols), :]
            send(part(pair_ref, f), dst, in_send.at[f], in_relay_recv.at[column, f], at)

        @pl.when(one_step)
        def _():
            at = device(to_column, to_chip, core)
            send(part(pair_ref, f), part(start_z, f), in_send.at[f], in_recv.at[f], at)

    @pl.when(stays)
    def _():
        start_z[...] = pair_ref[...]

    def each_relay(action):
        for b in range(COLUMNS):
            at_column, at_chip = placed(chip, b)
            here = jnp.logical_and(at_column == column, at_chip != chip)
            pl.when(jnp.logical_and(here, column != b))(functools.partial(action, b, at_chip))

    def relay_part(ref, b, f):
        return ref.at[b, :, pl.ds(f * part_cols, part_cols), :]

    for f in range(PARTS):

        def pass_in(b, at_chip):
            held = relay_part(relay_in, b, f)
            waiter(held, in_send.at[0], in_relay_recv.at[b, f]).wait_recv()
            at = device(column, at_chip, core)
            send(held, part(start_z, f), in_relay_send.at[b, f], in_recv.at[f], at)

        each_relay(pass_in)

    @pl.when(block != column)
    def _():
        waiter(valid_got, valid_send.at[0], valid_recv).wait_recv()

    def project(u, h, pair):
        there = pl.ds(h * cols, cols)
        valid = valid_got[0:1, h * cols : (h + 1) * cols]
        token = lax.broadcasted_iota(jnp.int32, (1, count), 1)

        def row(r, carry):
            z = pair[r, there, :].astype(F32)
            mean = jnp.mean(z, axis=1, keepdims=True)
            centered = z - mean
            var = jnp.mean(centered * centered, axis=1, keepdims=True)
            x = (centered * lax.rsqrt(var + EPSILON) * gain_ref[u, 0:1, :]).astype(BF16)
            normed[r, there, :] = x
            own = jnp.where(token == mine * rows + r, valid_got[0:1, :], 0.0)
            m = valid * jnp.sum(own, axis=1, keepdims=True)
            for k, store in ((2, right_f), (0, left_f)):
                gate = dot(wt[u, k * width : (k + 1) * width, :], x, 1, 1)
                value = dot(wt[u, (k + 1) * width : (k + 2) * width, :], x, 1, 1)
                edge = jax.nn.sigmoid(gate) * value * m
                for b in range(blocks_per_half):
                    store[h * blocks_per_half + b, pl.ds(r, width, stride=rows), :] = edge[
                        :, b * LANES : (b + 1) * LANES
                    ]
            return carry

        lax.fori_loop(0, rows, row, 0)

    def gate_values(u):
        def row(r, carry):
            gates[r] = jax.nn.sigmoid(dot(normed[r], proj_ref[u, :, 4 * width :], 1, 0))
            return carry

        lax.fori_loop(0, rows, row, 0)

    def packed(store, p, e, first, number):
        at = pl.ds(pl.multiple_of(p * tile + e * rows, rows), rows)
        return jnp.concatenate(
            [store[first + b, at, :] for b in range(number)], axis=1
        ).astype(BF16)

    def finish(u, h, pair, result):
        there = pl.ds(h * cols, cols)

        def unpack(p, carry):
            for e in range(2):
                at = pl.ds(pl.multiple_of(p * tile + e * rows, rows), rows)
                block = tri_in[u, h, e, p].astype(F32)
                for b in range(blocks_per_half):
                    tri_f[b, at, :] = block[:, b * LANES : (b + 1) * LANES]
            return carry

        lax.fori_loop(0, peers, unpack, 0, unroll=4)

        def row(r, carry):
            t = jnp.concatenate(
                [tri_f[b, pl.ds(r, width, stride=rows), :] for b in range(blocks_per_half)], axis=1
            )
            mean = jnp.mean(t, axis=0, keepdims=True)
            centered = t - mean
            var = jnp.mean(centered * centered, axis=0, keepdims=True)
            scaled = centered * lax.rsqrt(var + EPSILON)
            gain = jnp.concatenate([gain_col[u]] * blocks_per_half, axis=1)
            update = dot((scaled * gain).astype(BF16), wo_ref[u], 0, 0)
            z = pair[r, there, :].astype(F32)
            result[r, there, :] = (z + update * gates[r, there, :]).astype(BF16)
            return carry

        lax.fori_loop(0, rows, row, 0)

    def each_member(action):
        def step(k, carry):
            at_offset = (offset + side + k) % length
            for cc in (other, core):
                for i in range(COLUMNS):
                    at_column = (column + i) % COLUMNS
                    may_be_self = i == 0 and cc is core
                    action(at_column, at_offset, cc, k == side if may_be_self else None)
            return carry

        lax.fori_loop(0, length, step, 0)

    def send_or_keep(from_ref, to_ref, ssem, rsem, at, own):
        if own is None:
            send(from_ref, to_ref, ssem, rsem, at)
            return

        @pl.when(jnp.logical_not(own))
        def _():
            send(from_ref, to_ref, ssem, rsem, at)

        @pl.when(own)
        def _():
            to_ref[...] = from_ref[...]

    def scatter(u, h, e):
        def one(at_column, at_offset, at_core, own):
            at_owner = (at_offset * COLUMNS + at_column) * 2 + at_core
            send_or_keep(
                src.at[u, h, e, at_owner],
                land.at[u, h, e, mine],
                scat_send.at[u, h, e],
                scat_recv.at[u, h, e],
                device(at_column, length * block + at_offset, at_core),
                own,
            )

        each_member(one)

    def return_tri(u, e, h):
        def one(at_column, at_offset, at_core, own):
            at_rows = origin(at_column, at_offset) * 2 + at_core
            send_or_keep(
                tri_out.at[u, h, e, at_rows],
                tri_in.at[u, h, e, owner],
                tri_send.at[u, h, e],
                tri_recv.at[u, h, e],
                device(at_column, length * block + at_offset, at_core),
                own,
            )

        each_member(one)

    def edges(u, h, z):
        project(u, h, z)

        def pack(p, carry):
            for e in range(2):
                for kind, store in ((0, right_f), (1, left_f)):
                    src[u, h, e, p, kind] = packed(store, p, e, h * blocks_per_half, blocks_per_half)
            return carry

        lax.fori_loop(0, peers, pack, 0, unroll=2)
        for e in range(2):
            scatter(u, h, e)

    def multiply(u, e):
        for h in range(2):
            ref = land.at[u, h, e, pl.ds(0, peers - 1)]
            waiter(ref, scat_send.at[0, 0, 0], scat_recv.at[u, h, e]).wait_recv()

        def split(s, carry):
            at = pl.ds(pl.multiple_of(s * tile, tile), tile)
            for kind, mat in ((1, mat_l), (0, mat_r)):
                for h in range(2):
                    edge = land[u, h, e, pl.ds(2 * s, 2), kind].astype(F32)
                    mat[at, h * cols : (h + 1) * cols] = edge.reshape(tile, cols).astype(BF16)
            return carry

        lax.fori_loop(0, chips, split, 0)
        some = peers // 2
        for b in range(2):
            for h in range(2):
                first, second = slice(b * cols, (b + 1) * cols), slice(h * cols, (h + 1) * cols)
                if u == 0:
                    product = dot(mat_l[first, :], mat_r[second, :], 1, 1)
                else:
                    product = dot(mat_l[:, first], mat_r[:, second], 0, 0)
                tri_out[u, h, e, b * some : (b + 1) * some] = product.reshape(
                    some, rows, cols
                ).astype(BF16)

    def triangle(u):
        multiply(u, 0)
        return_tri(u, 0, 0)
        multiply(u, 1)
        return_tri(u, 1, 0)
        return_tri(u, 0, 1)
        return_tri(u, 1, 1)

    def arrived(u, h):
        for e in range(2):
            ref = tri_in.at[u, h, e, pl.ds(0, peers - 1)]
            waiter(ref, tri_send.at[0, 0, 0], tri_recv.at[u, h, e]).wait_recv()

    per_half = PARTS // 2

    for h in range(2):
        for f in range(h * per_half, (h + 1) * per_half):

            @pl.when(moves)
            def _():
                waiter(part(start_z, f), in_send.at[0], in_recv.at[f]).wait_recv()

        edges(0, h, start_z)
    gate_values(0)
    triangle(0)

    for h in range(2):
        arrived(0, h)
        finish(0, h, start_z, middle)
        edges(1, h, middle)
    gate_values(1)
    triangle(1)

    far = from_chip != chip
    away = jnp.logical_and(far, column != block)
    near = jnp.logical_and(moves, jnp.logical_not(away))
    for h in range(2):
        arrived(1, h)
        finish(1, h, middle, final_z)
        for f in range(h * per_half, (h + 1) * per_half):

            @pl.when(away)
            def _():
                at = device(column, from_chip, core)
                held = relay_part(relay_out, block, f)
                send(part(final_z, f), held, out_send.at[f], out_relay_recv.at[block, f], at)

            @pl.when(near)
            def _():
                at = device(block, from_chip, core)
                send(part(final_z, f), part(home_z, f), out_send.at[f], out_recv.at[f], at)

    for f in range(PARTS):

        def pass_out(b, at_chip):
            held = relay_part(relay_out, b, f)
            waiter(held, out_send.at[0], out_relay_recv.at[b, f]).wait_recv()
            at = device(b, chip, core)
            send(held, part(home_z, f), out_relay_send.at[b, f], out_recv.at[f], at)

        each_relay(pass_out)

    for f in range(PARTS):
        there = pl.ds(f * part_cols, part_cols)

        @pl.when(moves)
        def _():
            waiter(part(home_z, f), out_send.at[0], out_recv.at[f]).wait_recv()
            out_ref[:, there, :] = home_z[:, there, :]

        @pl.when(stays)
        def _():
            out_ref[:, there, :] = final_z[:, there, :]

    @pl.when(block == column)
    def _():
        for i in range(1, COLUMNS):
            waiter(valid_own, valid_send.at[i - 1], valid_recv).wait_send()

    @pl.when(moves)
    def _():
        for f in range(PARTS):
            waiter(part(pair_ref, f), in_send.at[f], in_recv.at[f]).wait_send()
            waiter(part(final_z, f), out_send.at[f], out_recv.at[f]).wait_send()

    def left_relay(b, at_chip):
        for f in range(PARTS):
            waiter(relay_part(relay_in, b, f), in_relay_send.at[b, f], in_recv.at[f]).wait_send()
            waiter(relay_part(relay_out, b, f), out_relay_send.at[b, f], out_recv.at[f]).wait_send()

    each_relay(left_relay)
    for u in range(2):
        for h in range(2):
            for e in range(2):
                waiter(
                    src.at[u, h, e, pl.ds(0, peers - 1)], scat_send.at[u, h, e], scat_recv.at[u, h, e]
                ).wait_send()
                waiter(
                    tri_out.at[u, h, e, pl.ds(0, peers - 1)], tri_send.at[u, h, e], tri_recv.at[u, h, e]
                ).wait_send()


def per_device(peers, across, pair_in, valid_tokens, proj_weight, out_weight, norm_gains):
    rows, count, width = pair_in.shape
    cols = count // 2
    vmem = pltpu.VMEM
    dma = pltpu.SemaphoreType.DMA
    pair = vmem((rows, count, width), BF16)
    relayed = vmem((COLUMNS, rows, count, width), BF16)
    edge_tiles = vmem((2, 2, 2, peers, 2, rows, cols), BF16)
    tri_tiles = vmem((2, 2, 2, peers, rows, cols), BF16)
    whole = pl.BlockSpec(memory_space=pltpu.VMEM)
    return pl.pallas_call(
        functools.partial(kernel, peers, across),
        out_shape=jax.ShapeDtypeStruct((rows, count, width), BF16),
        in_specs=[whole] * 5,
        out_specs=whole,
        scratch_shapes=[
            vmem((2, 4 * width, width), BF16),
            vmem((2, width, width), F32),
            vmem((count // LANES, width * rows, LANES), F32),
            vmem((count // LANES, width * rows, LANES), F32),
            vmem((cols // LANES, width * rows, LANES), F32),
            pair,
            vmem((rows, count, width), F32),
            vmem((8, count), F32),
            vmem((8, count), F32),
            pair,
            pair,
            pair,
            pair,
            relayed,
            relayed,
            edge_tiles,
            edge_tiles,
            vmem((count, count), BF16),
            vmem((count, count), BF16),
            tri_tiles,
            tri_tiles,
            dma((COLUMNS - 1,)),
            dma,
            dma((PARTS,)),
            dma((PARTS,)),
            dma((COLUMNS, PARTS)),
            dma((COLUMNS, PARTS)),
            dma((PARTS,)),
            dma((PARTS,)),
            dma((COLUMNS, PARTS)),
            dma((COLUMNS, PARTS)),
            dma((2, 2, 2)),
            dma((2, 2, 2)),
            dma((2, 2, 2)),
            dma((2, 2, 2)),
        ],
        compiler_params=pltpu.CompilerParams(
            collective_id=0, has_side_effects=True, vmem_limit_bytes=60 * 1024 * 1024
        ),
    )(pair_in, valid_tokens.reshape(1, count), proj_weight, out_weight, norm_gains)


def solution(mesh):
    across = len({d.coords[0] for d in mesh.devices[:, 0]})
    return jax.shard_map(
        functools.partial(per_device, mesh.shape["row"], across),
        mesh=mesh,
        in_specs=(P(("groups", "row"), None, None), P("groups"), P(), P(), P()),
        out_specs=P(("groups", "row"), None, None),
        check_vma=False,
    )
```

time: 714 us -> 538 us (0.75)
  the two profiles are of different devices: /device:TPU:44 before, /device:TPU:750 now
where the time goes in v4:
time: 538 us
  Pallas kernels  536 us (100%)
    pallas_call x1, Pallas kernels, per_device(): pl.pallas_call(functools.partial(kernel, peers, across), out_shape=jax.Sh...  536 us

profile of v4, /device:TPU:750, one launch (start us, length us, event | category | flops | bytes accessed | tf_op | source)
XLA Modules:
  0.0 538.2 jit_solution(2176458301438357147)
XLA Ops:
  0.0 536.0 %shard_map.55 = bf16[8,512,128]{2,1,0:T(8,128)(2,1)} custom-call(bf16[8,512,128]{2,1,0:T(8,128)(2,1)} %pair_ref.1, s32[1,512]{1,0:T(1,128)} %bitcast.1, bf16[2,128,640]{2,1,0:T(8,128)(2,1)} %proj_ref.1, bf16[2,128,128]{2,1,0:T(8,128)(2,1)} %wo_ref.1, f32[2,2,128]{2,1,0:T(2,128)} %gain_ref.1), custom_call_target="tpu_custom_call" | custom-call | tf_op jit(solution)/shard_map/pallas_call | solution.py:497
  536.0 2.3 copy.7

commit v5 on v4

--- a/solution.py
+++ b/solution.py
@@ -10,7 +10,6 @@
 MESH = pl.DeviceIdType.MESH
 EPSILON = 1e-05
 COLUMNS = 4
-PARTS = 4
 LANES = 128
 BF16 = jnp.bfloat16
 F32 = jnp.float32
@@ -66,6 +65,7 @@
     scat_recv,
     tri_send,
     tri_recv,
+    calm,
 ):
     rows, count, width = pair_ref.shape
     chips = peers // 2
@@ -73,7 +73,8 @@
     side = length // 2
     outer = (chips - length) // 2
     cols = count // 2
-    part_cols = count // PARTS
+    part_cols = LANES
+    parts = count // LANES
     blocks_per_half = cols // LANES
     tile = 2 * rows
     me = lax.axis_index("row")
@@ -114,15 +115,16 @@
         t = (at_chip - length * of_group + outer + chips) % chips - outer
         half = (t + outer) // (2 * length)
         a = mirror(half, t) + outer
-        at_column = a % COLUMNS
-        w = (at_column + 1 + a // COLUMNS) % COLUMNS
-        return at_column, length * of_group + mirror(half, w)
+        turn = a % COLUMNS
+        w = (turn + 1 + a // COLUMNS) % COLUMNS
+        return (turn + of_group) % COLUMNS, length * of_group + mirror(half, w)
 
     def origin(at_column, at_offset):
         half = at_offset // side
         w = mirror(half, at_offset)
-        k = (w - at_column - 1 + 2 * COLUMNS) % COLUMNS
-        t = mirror(half, COLUMNS * k + at_column - outer)
+        turn = (at_column - block + COLUMNS) % COLUMNS
+        k = (w - turn - 1 + 2 * COLUMNS) % COLUMNS
+        t = mirror(half, COLUMNS * k + turn - outer)
         return (length * block + t + chips) % chips
 
     to_column, to_chip = placed(chip, column)
@@ -182,7 +184,7 @@
             send(valid_own, valid_got, valid_send.at[i - 1], valid_recv, at)
         valid_got[...] = valid_own[...]
 
-    for f in range(PARTS):
+    for f in range(parts):
 
         @pl.when(two_steps)
         def _():
@@ -208,7 +210,7 @@
     def relay_part(ref, b, f):
         return ref.at[b, :, pl.ds(f * part_cols, part_cols), :]
 
-    for f in range(PARTS):
+    for f in range(parts):
 
         def pass_in(b, at_chip):
             held = relay_part(relay_in, b, f)
@@ -222,9 +224,9 @@
     def _():
         waiter(valid_got, valid_send.at[0], valid_recv).wait_recv()
 
-    def project(u, h, pair):
-        there = pl.ds(h * cols, cols)
-        valid = valid_got[0:1, h * cols : (h + 1) * cols]
+    def project(u, first, number, pair):
+        there = pl.ds(first * LANES, number * LANES)
+        valid = valid_got[0:1, first * LANES : (first + number) * LANES]
         token = lax.broadcasted_iota(jnp.int32, (1, count), 1)
 
         def row(r, carry):
@@ -240,8 +242,8 @@
                 gate = dot(wt[u, k * width : (k + 1) * width, :], x, 1, 1)
                 value = dot(wt[u, (k + 1) * width : (k + 2) * width, :], x, 1, 1)
                 edge = jax.nn.sigmoid(gate) * value * m
-                for b in range(blocks_per_half):
-                    store[h * blocks_per_half + b, pl.ds(r, width, stride=rows), :] = edge[
+                for b in range(number):
+                    store[first + b, pl.ds(r, width, stride=rows), :] = edge[
                         :, b * LANES : (b + 1) * LANES
                     ]
             return carry
@@ -254,12 +256,6 @@
             return carry
 
         lax.fori_loop(0, rows, row, 0)
-
-    def packed(store, p, e, first, number):
-        at = pl.ds(pl.multiple_of(p * tile + e * rows, rows), rows)
-        return jnp.concatenate(
-            [store[first + b, at, :] for b in range(number)], axis=1
-        ).astype(BF16)
 
     def finish(u, h, pair, result):
         there = pl.ds(h * cols, cols)
@@ -315,12 +311,14 @@
         def _():
             to_ref[...] = from_ref[...]
 
-    def scatter(u, h, e):
+    def scatter(u, h, e, q):
         def one(at_column, at_offset, at_core, own):
             at_owner = (at_offset * COLUMNS + at_column) * 2 + at_core
+            from_ref = src.at[u, h, e, at_owner]
+            to_ref = land.at[u, h, e, mine]
             send_or_keep(
-                src.at[u, h, e, at_owner],
-                land.at[u, h, e, mine],
+                from_ref if q is None else from_ref.at[q],
+                to_ref if q is None else to_ref.at[q],
                 scat_send.at[u, h, e],
                 scat_recv.at[u, h, e],
                 device(at_column, length * block + at_offset, at_core),
@@ -343,18 +341,21 @@
 
         each_member(one)
 
-    def edges(u, h, z):
-        project(u, h, z)
+    def edges(u, first, number, z):
+        project(u, first, number, z)
+        h = first // blocks_per_half
 
         def pack(p, carry):
             for e in range(2):
-                for kind, store in ((0, right_f), (1, left_f)):
-                    src[u, h, e, p, kind] = packed(store, p, e, h * blocks_per_half, blocks_per_half)
+                at = pl.ds(pl.multiple_of(p * tile + e * rows, rows), rows)
+                for b in range(first, first + number):
+                    for kind, store in ((0, right_f), (1, left_f)):
+                        src[u, h, e, p, b % blocks_per_half, kind] = store[b, at, :].astype(BF16)
             return carry
 
         lax.fori_loop(0, peers, pack, 0, unroll=2)
         for e in range(2):
-            scatter(u, h, e)
+            scatter(u, h, e, None if number == blocks_per_half else first % blocks_per_half)
 
     def multiply(u, e):
         for h in range(2):
@@ -364,9 +365,10 @@
         def split(s, carry):
             at = pl.ds(pl.multiple_of(s * tile, tile), tile)
             for kind, mat in ((1, mat_l), (0, mat_r)):
-                for h in range(2):
-                    edge = land[u, h, e, pl.ds(2 * s, 2), kind].astype(F32)
-                    mat[at, h * cols : (h + 1) * cols] = edge.reshape(tile, cols).astype(BF16)
+                for b in range(2 * blocks_per_half):
+                    h, q = b // blocks_per_half, b % blocks_per_half
+                    edge = land[u, h, e, pl.ds(2 * s, 2), q, kind].astype(F32)
+                    mat[at, b * LANES : (b + 1) * LANES] = edge.reshape(tile, LANES).astype(BF16)
             return carry
 
         lax.fori_loop(0, chips, split, 0)
@@ -395,32 +397,41 @@
             ref = tri_in.at[u, h, e, pl.ds(0, peers - 1)]
             waiter(ref, tri_send.at[0, 0, 0], tri_recv.at[u, h, e]).wait_recv()
 
-    per_half = PARTS // 2
-
-    for h in range(2):
-        for f in range(h * per_half, (h + 1) * per_half):
-
-            @pl.when(moves)
-            def _():
-                waiter(part(start_z, f), in_send.at[0], in_recv.at[f]).wait_recv()
-
-        edges(0, h, start_z)
+    per_half = parts // 2
+
+    for f in range(parts):
+
+        @pl.when(moves)
+        def _():
+            waiter(part(start_z, f), in_send.at[0], in_recv.at[f]).wait_recv()
+
+        edges(0, f, 1, start_z)
     gate_values(0)
     triangle(0)
 
     for h in range(2):
         arrived(0, h)
         finish(0, h, start_z, middle)
-        edges(1, h, middle)
+        edges(1, h * blocks_per_half, blocks_per_half, middle)
     gate_values(1)
     triangle(1)
 
     far = from_chip != chip
     away = jnp.logical_and(far, column != block)
     near = jnp.logical_and(moves, jnp.logical_not(away))
+    arrived(1, 0)
+    finish(1, 0, middle, final_z)
+    arrived(1, 1)
+
+    def tell(k, carry):
+        at = device(column, (chip + 1 + k) % chips, core)
+        pl.semaphore_signal(calm, inc=1, device_id=at, device_id_type=MESH)
+        return carry
+
+    lax.fori_loop(0, chips - 1, tell, 0)
+    finish(1, 1, middle, final_z)
+    pl.semaphore_wait(calm, chips - 1)
     for h in range(2):
-        arrived(1, h)
-        finish(1, h, middle, final_z)
         for f in range(h * per_half, (h + 1) * per_half):
 
             @pl.when(away)
@@ -434,7 +445,7 @@
                 at = device(block, from_chip, core)
                 send(part(final_z, f), part(home_z, f), out_send.at[f], out_recv.at[f], at)
 
-    for f in range(PARTS):
+    for f in range(parts):
 
         def pass_out(b, at_chip):
             held = relay_part(relay_out, b, f)
@@ -444,7 +455,7 @@
 
         each_relay(pass_out)
 
-    for f in range(PARTS):
+    for f in range(parts):
         there = pl.ds(f * part_cols, part_cols)
 
         @pl.when(moves)
@@ -463,12 +474,12 @@
 
     @pl.when(moves)
     def _():
-        for f in range(PARTS):
+        for f in range(parts):
             waiter(part(pair_ref, f), in_send.at[f], in_recv.at[f]).wait_send()
             waiter(part(final_z, f), out_send.at[f], out_recv.at[f]).wait_send()
 
     def left_relay(b, at_chip):
-        for f in range(PARTS):
+        for f in range(parts):
             waiter(relay_part(relay_in, b, f), in_relay_send.at[b, f], in_recv.at[f]).wait_send()
             waiter(relay_part(relay_out, b, f), out_relay_send.at[b, f], out_recv.at[f]).wait_send()
 
@@ -491,7 +502,8 @@
     dma = pltpu.SemaphoreType.DMA
     pair = vmem((rows, count, width), BF16)
     relayed = vmem((COLUMNS, rows, count, width), BF16)
-    edge_tiles = vmem((2, 2, 2, peers, 2, rows, cols), BF16)
+    parts = count // LANES
+    edge_tiles = vmem((2, 2, 2, peers, parts // 2, 2, rows, LANES), BF16)
     tri_tiles = vmem((2, 2, 2, peers, rows, cols), BF16)
     whole = pl.BlockSpec(memory_space=pltpu.VMEM)
     return pl.pallas_call(
@@ -523,18 +535,19 @@
             tri_tiles,
             dma((COLUMNS - 1,)),
             dma,
-            dma((PARTS,)),
-            dma((PARTS,)),
-            dma((COLUMNS, PARTS)),
-            dma((COLUMNS, PARTS)),
-            dma((PARTS,)),
-            dma((PARTS,)),
-            dma((COLUMNS, PARTS)),
-            dma((COLUMNS, PARTS)),
+            dma((parts,)),
+            dma((parts,)),
+            dma((COLUMNS, parts)),
+            dma((COLUMNS, parts)),
+            dma((parts,)),
+            dma((parts,)),
+            dma((COLUMNS, parts)),
+            dma((COLUMNS, parts)),
             dma((2, 2, 2)),
             dma((2, 2, 2)),
             dma((2, 2, 2)),
             dma((2, 2, 2)),
+            pltpu.SemaphoreType.REGULAR,
         ],
         compiler_params=pltpu.CompilerParams(
             collective_id=0, has_side_effects=True, vmem_limit_bytes=60 * 1024 * 1024

time: 538 us -> 502 us (0.933)
  the two profiles are of different devices: /device:TPU:750 before, /device:TPU:44 now
where the time goes in v5:
time: 502 us
  Pallas kernels  499 us (99%)
    pallas_call x1, Pallas kernels, per_device(): pl.pallas_call(functools.partial(kernel, peers, across), out_shape=jax.Sh...  499 us

profile of v5, /device:TPU:44, one launch (start us, length us, event | category | flops | bytes accessed | tf_op | source)
XLA Modules:
  0.0 501.7 jit_solution(5617461959028281160)
XLA Ops:
  0.0 499.4 %shard_map.55 = bf16[8,512,128]{2,1,0:T(8,128)(2,1)} custom-call(bf16[8,512,128]{2,1,0:T(8,128)(2,1)} %pair_ref.1, s32[1,512]{1,0:T(1,128)} %bitcast.1, bf16[2,128,640]{2,1,0:T(8,128)(2,1)} %proj_ref.1, bf16[2,128,128]{2,1,0:T(8,128)(2,1)} %wo_ref.1, f32[2,2,128]{2,1,0:T(2,128)} %gain_ref.1), custom_call_target="tpu_custom_call" | custom-call | tf_op jit(solution)/shard_map/pallas_call | solution.py:509
  499.4 2.3 copy.7

commit v6 on v5

--- a/solution.py
+++ b/solution.py
@@ -420,8 +420,6 @@
     away = jnp.logical_and(far, column != block)
     near = jnp.logical_and(moves, jnp.logical_not(away))
     arrived(1, 0)
-    finish(1, 0, middle, final_z)
-    arrived(1, 1)
 
     def tell(k, carry):
         at = device(column, (chip + 1 + k) % chips, core)
@@ -429,6 +427,8 @@
         return carry
 
     lax.fori_loop(0, chips - 1, tell, 0)
+    finish(1, 0, middle, final_z)
+    arrived(1, 1)
     finish(1, 1, middle, final_z)
     pl.semaphore_wait(calm, chips - 1)
     for h in range(2):

time: 502 us -> 492 us (0.980)
  Pallas kernels: 499 us -> 489 us
    pallas_call x1, Pallas kernels: 499 us -> 489 us  [per_device(): pl.pallas_call(functools.partial(kernel, peers, across), out_shape=jax.Sh...]
where the time goes in v6:
time: 492 us
  Pallas kernels  489 us (99%)
    pallas_call x1, Pallas kernels, per_device(): pl.pallas_call(functools.partial(kernel, peers, across), out_shape=jax.Sh...  489 us

profile of v6, /device:TPU:44, one launch (start us, length us, event | category | flops | bytes accessed | tf_op | source)
XLA Modules:
  0.0 491.8 jit_solution(8129831260291996730)
XLA Ops:
  0.0 489.5 %shard_map.55 = bf16[8,512,128]{2,1,0:T(8,128)(2,1)} custom-call(bf16[8,512,128]{2,1,0:T(8,128)(2,1)} %pair_ref.1, s32[1,512]{1,0:T(1,128)} %bitcast.1, bf16[2,128,640]{2,1,0:T(8,128)(2,1)} %proj_ref.1, bf16[2,128,128]{2,1,0:T(8,128)(2,1)} %wo_ref.1, f32[2,2,128]{2,1,0:T(2,128)} %gain_ref.1), custom_call_target="tpu_custom_call" | custom-call | tf_op jit(solution)/shard_map/pallas_call | solution.py:509
  489.5 2.3 copy.7
